TPU v7x, 32 devices: a whole 2x2x4 slice. The times are simulated.
32 devices in a mesh: rep: 4 (over x, y), dp: 8 (over z, core).
Axes of the slice: x: 2, y: 2, z: 4, core: 2. Of those that a mesh axis runs over, the one named last changes fastest.
Arguments:
- x: bfloat16 [32, 4096, 512], P(('rep', 'dp')), parts along dimension 0
- dy: bfloat16 [32, 4096, 512], P(('rep', 'dp')), parts along dimension 0
- w_gate: bfloat16 [2, 512, 1664], P(None, 'dp')
- w_up: bfloat16 [2, 512, 1664], P(None, 'dp')
- w_down: bfloat16 [2, 1664, 512], P(None, 'dp')
- m_w_gate: float32 [2, 512, 1664], P(None, 'dp')
- m_w_up: float32 [2, 512, 1664], P(None, 'dp')
- m_w_down: float32 [2, 1664, 512], P(None, 'dp')
- v_w_gate: float32 [2, 512, 1664], P(None, 'dp')
- v_w_up: float32 [2, 512, 1664], P(None, 'dp')
- v_w_down: float32 [2, 1664, 512], P(None, 'dp')
Outputs:
- output 1: bfloat16 [8, 512, 1664], P('rep', 'dp'), parts along dimension 0
- output 2: bfloat16 [8, 512, 1664], P('rep', 'dp'), parts along dimension 0
- output 3: bfloat16 [8, 1664, 512], P('rep', 'dp'), parts along dimension 0
- output 4: float32 [8, 512, 1664], P('rep', 'dp'), parts along dimension 0
- output 5: float32 [8, 512, 1664], P('rep', 'dp'), parts along dimension 0
- output 6: float32 [8, 1664, 512], P('rep', 'dp'), parts along dimension 0
- output 7: float32 [8, 512, 1664], P('rep', 'dp'), parts along dimension 0
- output 8: float32 [8, 512, 1664], P('rep', 'dp'), parts along dimension 0
- output 9: float32 [8, 1664, 512], P('rep', 'dp'), parts along dimension 0
There are 4 independent parts. A program takes and returns all parts, laid end to end along the dimension named above; an argument that names none is the same for every part.
All inputs are finite; a program needn't handle non-finite values.
Results may differ from a plain program's by a relative error of at most 0.02.
Values are sent between devices in bfloat16 or wider.
A program may use at most 2 GiB of HBM per device.

v0:
```python
import jax
import jax.numpy as jnp
from jax import lax
from jax.sharding import PartitionSpec as P

NAMES = ("w_gate", "w_up", "w_down")


def matmul(a, w):
    return jnp.dot(a, w, preferred_element_type=jnp.float32).astype(jnp.bfloat16)


def normed(h):
    wide = h.astype(jnp.float32)
    scale = lax.rsqrt(jnp.mean(wide**2, -1, keepdims=True) + 1e-6)
    return (wide * scale).astype(jnp.bfloat16)


def layer(h, w):
    a = normed(h)
    gate = jnp.dot(a, w["w_gate"], preferred_element_type=jnp.float32)
    up = jnp.dot(a, w["w_up"], preferred_element_type=jnp.float32)
    return h + matmul((jax.nn.silu(gate) * up).astype(jnp.bfloat16), w["w_down"])


def adamw(w, m, v, g):
    m = 0.9 * m + 0.1 * g
    v = 0.95 * v + 0.05 * g * g
    step = m * lax.rsqrt(v + 1e-8) + 0.1 * w
    return (w - 0.02 * step).astype(jnp.bfloat16), m, v


def solution(mesh):
    def fetched(weights, number):
        return {name: lax.all_gather(w[number], "dp", axis=0, tiled=True) for name, w in zip(NAMES, weights, strict=True)}

    def step(x, dy, *arrays):
        weights, m, v = (arrays[i : i + 3] for i in (0, 3, 6))
        layers = weights[0].shape[0]
        h, kept = x[0], []
        for number in range(layers):
            kept.append(h)
            h = layer(h, fetched(weights, number))
        by_h, mine = dy[0], [None] * layers
        for number in reversed(range(layers)):
            _, back = jax.vjp(lambda w, h: layer(h, w), fetched(weights, number), kept[number])
            by_w, by_h = back(by_h)
            mine[number] = [lax.psum_scatter(by_w[name], "dp", scatter_dimension=0, tiled=True) for name in NAMES]
        gradients = [jnp.stack([mine[number][i] for number in range(layers)]).astype(jnp.float32) for i in range(3)]
        new = [adamw(w.astype(jnp.float32), m, v, g) for w, m, v, g in zip(weights, m, v, gradients, strict=True)]
        return tuple(one[which] for which in range(3) for one in new)

    states, cut = P(("rep", "dp"), None, None), P(None, "dp", None)
    return jax.shard_map(
        step,
        mesh=mesh,
        in_specs=(states, states) + (cut,) * 9,
        out_specs=(P("rep", "dp", None),) * 9,
        check_vma=False,
    )
```

profile of v0, /device:TPU:0, one launch (start us, length us, event | category | flops | bytes accessed | tf_op | source)
XLA Modules:
  0.0 486.2 jit_solution(12141289125355773352)
XLA Ops:
  7.2 0.0 all-gather.13.cloned.1.call-start
  7.2 1.8 fusion.87
  9.1 0.0 all-gather.15.cloned.1.call-start
  9.1 1.8 fusion.86
  11.0 0.0 all-gather.17.cloned.1.call-start
  11.0 1.8 fusion.85
  12.9 0.0 all-gather.21.cloned.1.call-start
  12.9 0.5 all-gather.21.cloned.1.call-update
  13.4 0.0 all-gather.23.cloned.1.call-start
  13.5 0.5 all-gather.23.cloned.1.call-update
  14.1 0.5 all-gather.19.cloned.1.call-update
  14.6 0.0 reduce-scatter.9.cloned.1.call-start
  14.6 6.5 %copy.20 = bf16[1,4096,512]{1,2,0:T(8,128)(2,1)} copy(bf16[1,4096,512]{2,1,0:T(8,128)(2,1)} %param.11) | data formatting | bytes 8388608 | tf_op args[0]
  21.1 3.1 fusion.15
  24.2 6.5 %copy.21 = bf16[1,4096,512]{1,2,0:T(8,128)(2,1)} copy(bf16[1,4096,512]{2,1,0:T(8,128)(2,1)} %param.12) | data formatting | bytes 8388608 | tf_op args[1]
  30.7 8.4 %all-gather.13.cloned.1.call-done = bf16[1,512,1664]{2,1,0:T(8,128)(2,1)} async-done(((bf16[1,64,1664]{2,1,0:T(8,128)(2,1)}), bf16[1,512,1664]{2,1,0:T(8,128)(2,1)}) %all-gather.13.cloned.1.call-update) | async-done | bytes 1703952 | tf_op jit(solution)/shard_map/all_gather | solution.py:35
  39.1 15.1 %fusion.47 = f32[4096,1664]{1,0:T(8,128)} fusion(bf16[1,4096,512]{1,2,0:T(8,128)(2,1)} %copy.20, f32[4096]{0:T(1024)S(1)} %add_rsqrt_fusion, bf16[1,512,1664]{2,1,0:T(8,128)(2,1)} %all-gather.13.cloned.1.call-done), kind=kOutput, calls=%fused_computation.57 | convolution fusion | flops 6985613312 | bytes 33177600 | tf_op jit(solution)/shard_map/dot_general | solution.py:21
  54.3 12.4 %all-gather.15.cloned.1.call-done = bf16[1,512,1664]{2,1,0:T(8,128)(2,1)} async-done(((bf16[1,64,1664]{2,1,0:T(8,128)(2,1)}), bf16[1,512,1664]{2,1,0:T(8,128)(2,1)}) %all-gather.15.cloned.1.call-update) | async-done | bytes 1703952 | tf_op jit(solution)/shard_map/all_gather | solution.py:35
  66.7 27.6 %multiply_convert_fusion.1 = (bf16[4096,1664]{1,0:T(8,128)(2,1)}, f32[4096,1664]{1,0:T(8,128)}) fusion(f32[4096,1664]{1,0:T(8,128)} %fusion.47, bf16[1,512,1664]{2,1,0:T(8,128)(2,1)} %all-gather.15.cloned.1.call-done, bf16[1,4096,512]{1,2,0:T(8,128)(2,1)} %copy.20, f32[4096]{0:T(1024)S(1)} %add_rsqrt_fusion), kind=kOutput, calls=%fused_computation.17 | convolution fusion | flops 7026507776 | bytes 74072064 | tf_op jit(solution)/shard_map/dot_general | solution.py:22
  94.3 14.2 %fusion.19 = (f32[4096]{0:T(1024)S(1)}, bf16[4096,512]{0,1:T(8,128)(2,1)}) fusion(bf16[4096,1664]{1,0:T(8,128)(2,1)} %get-tuple-element.24, bf16[1,1664,512]{2,1,0:T(8,128)(2,1)} %all-gather.17.cloned.1.call-done, bf16[1,4096,512]{1,2,0:T(8,128)(2,1)} %copy.20), kind=kOutput, calls=%fused_computation.37 | convolution fusion | flops 6989803520 | bytes 23740416 | tf_op jit(solution)/shard_map/dot_general | solution.py:10
  108.6 0.6 copy-done.9
  109.2 12.5 %all-gather.21.cloned.1.call-done = bf16[1,1664,512]{2,1,0:T(8,128)(2,1)} async-done(((bf16[1,208,512]{2,1,0:T(8,128)(2,1)}), bf16[1,1664,512]{2,1,0:T(8,128)(2,1)}) %all-gather.21.cloned.1.call-update) | async-done | bytes 1703952 | tf_op jit(solution)/shard_map/all_gather | solution.py:35
  121.7 12.9 %convolution_convert_fusion.1 = bf16[4096,1664]{1,0:T(8,128)(2,1)} fusion(bf16[1,4096,512]{2,1,0:T(8,128)(2,1)} %param.12, bf16[1,1664,512]{2,1,0:T(8,128)(2,1)} %all-gather.21.cloned.1.call-done), kind=kOutput, calls=%fused_computation.23 | convolution fusion | flops 6986137600 | bytes 19529728 | tf_op jit(solution)/shard_map/transpose(jvp())/dot_general | solution.py:10
  134.5 14.5 %all-gather.23.cloned.1.call-done = bf16[1,512,1664]{2,1,0:T(8,128)(2,1)} async-done(((bf16[1,64,1664]{2,1,0:T(8,128)(2,1)}), bf16[1,512,1664]{2,1,0:T(8,128)(2,1)}) %all-gather.23.cloned.1.call-update) | async-done | bytes 1703952 | tf_op jit(solution)/shard_map/all_gather | solution.py:35
  149.1 15.0 %fusion.39 = f32[4096,1664]{1,0:T(8,128)} fusion(bf16[4096,512]{0,1:T(8,128)(2,1)} %get-tuple-element.27, f32[4096]{0:T(1024)S(1)} %fusion.73, bf16[1,512,1664]{2,1,0:T(8,128)(2,1)} %all-gather.23.cloned.1.call-done), kind=kOutput, calls=%fused_computation.54 | convolution fusion | flops 6985613312 | bytes 33177600 | tf_op jit(solution)/shard_map/jvp()/dot_general | solution.py:22
  164.1 12.4 %all-gather.19.cloned.1.call-done = bf16[1,512,1664]{2,1,0:T(8,128)(2,1)} async-done(((bf16[1,64,1664]{2,1,0:T(8,128)(2,1)}), bf16[1,512,1664]{2,1,0:T(8,128)(2,1)}) %all-gather.19.cloned.1.call-update) | async-done | bytes 1703952 | tf_op jit(solution)/shard_map/all_gather | solution.py:35
  176.5 36.8 %fusion.2 = (bf16[4096,1664]{1,0:T(8,128)(2,1)}, f32[4096,1664]{1,0:T(8,128)}) fusion(f32[4096,1664]{1,0:T(8,128)} %fusion.39, bf16[4096,1664]{1,0:T(8,128)(2,1)} %convolution_convert_fusion.1, bf16[1,512,1664]{2,1,0:T(8,128)(2,1)} %all-gather.19.cloned.1.call-done, bf16[4096,512]{0,1:T(8,128)(2,1)} %get-tuple-element.27, f32[4096]{0:T(1024)S(1)} %fusion.73), kind=kOutput, calls=%fused_computation.8 | convolution fusion | flops 7067402240 | bytes 87703552 | tf_op jit(solution)/shard_map/jvp()/dot_general | solution.py:21
  213.3 14.5 %convolution_convert_fusion.4 = bf16[512,1664]{1,0:T(8,128)(2,1)} fusion(bf16[4096,1664]{1,0:T(8,128)(2,1)} %get-tuple-element.28, bf16[4096,512]{0,1:T(8,128)(2,1)} %get-tuple-element.27, f32[4096]{0:T(1024)S(1)} %fusion.73), kind=kOutput, calls=%fused_computation.49 | convolution fusion | flops 6985613312 | bytes 19546112 | tf_op jit(solution)/shard_map/transpose(jvp())/dot_general | solution.py:21
  227.8 0.0 reduce-scatter.7.cloned.1.call-start
  227.9 19.3 %fusion.22 = bf16[4096,512]{0,1:T(8,128)(2,1)} fusion(bf16[4096,1664]{1,0:T(8,128)(2,1)} %convolution_convert_fusion.1, bf16[1,512,1664]{2,1,0:T(8,128)(2,1)S(1)} %copy-done.14, f32[4096,1664]{1,0:T(8,128)} %get-tuple-element.29), kind=kOutput, calls=%fused_computation.40 | convolution fusion | flops 7022313472 | bytes 46792704 | tf_op jit(solution)/shard_map/transpose(jvp())/dot_general | solution.py:22
  247.2 13.7 %fusion.21 = (f32[4096]{0:T(1024)S(1)}, bf16[4096,512]{0,1:T(8,128)(2,1)S(1)}) fusion(bf16[4096,512]{0,1:T(8,128)(2,1)} %get-tuple-element.27, bf16[4096,512]{0,1:T(8,128)(2,1)} %fusion.22, bf16[4096,1664]{1,0:T(8,128)(2,1)} %get-tuple-element.28, bf16[1,512,1664]{2,1,0:T(8,128)(2,1)} %all-gather.19.cloned.1.call-done), kind=kOutput, calls=%fused_computation.39 | convolution fusion | flops 6989803520 | bytes 27934720 | tf_op jit(solution)/shard_map/transpose(jvp())/dot_general | solution.py:21
  261.0 3.1 fusion.26
  264.2 11.2 %convolution_convert_fusion = bf16[4096,1664]{1,0:T(8,128)(2,1)} fusion(bf16[4096,512]{0,1:T(8,128)(2,1)S(1)} %fusion.26, bf16[1,1664,512]{2,1,0:T(8,128)(2,1)S(1)} %copy-done.13), kind=kOutput, calls=%fused_computation.22 | convolution fusion | flops 6986137600 | bytes 19529728 | tf_op jit(solution)/shard_map/transpose(jvp())/dot_general | solution.py:10
  275.4 25.7 %fusion.34 = bf16[512,1664]{1,0:T(8,128)(2,1)} fusion(f32[4096,1664]{1,0:T(8,128)} %fusion.47, f32[4096,1664]{1,0:T(8,128)} %get-tuple-element.25, bf16[4096,1664]{1,0:T(8,128)(2,1)} %convolution_convert_fusion, bf16[1,4096,512]{1,2,0:T(8,128)(2,1)S(1)} %copy-done, f32[4096]{0:T(1024)S(1)} %copy-done.12), kind=kOutput, calls=%fused_computation.53 | convolution fusion | flops 7061438464 | bytes 74072064 | tf_op jit(solution)/shard_map/transpose(jvp())/dot_general | solution.py:21
  301.1 0.0 reduce-scatter.13.cloned.1.call-start
  301.2 20.2 %fusion.33 = bf16[512,1664]{1,0:T(8,128)(2,1)} fusion(bf16[4096,1664]{1,0:T(8,128)(2,1)} %convolution_convert_fusion.1, bf16[4096,512]{0,1:T(8,128)(2,1)} %get-tuple-element.27, f32[4096]{0:T(1024)S(1)} %fusion.73, f32[4096,1664]{1,0:T(8,128)} %get-tuple-element.29), kind=kOutput, calls=%fused_computation.51 | convolution fusion | flops 7027359744 | bytes 46809088 | tf_op jit(solution)/shard_map/transpose(jvp())/dot_general | solution.py:22
  321.4 0.0 reduce-scatter.11.cloned.1.call-start
  321.4 19.8 %fusion.29 = bf16[512,1664]{1,0:T(8,128)(2,1)} fusion(bf16[4096,1664]{1,0:T(8,128)(2,1)} %convolution_convert_fusion, f32[4096,1664]{1,0:T(8,128)} %fusion.47, bf16[1,4096,512]{1,2,0:T(8,128)(2,1)} %copy.20, f32[4096]{0:T(1024)S(1)} %copy-done.12), kind=kOutput, calls=%fused_computation.48 | convolution fusion | flops 7027359744 | bytes 46809088 | tf_op jit(solution)/shard_map/transpose(jvp())/dot_general | solution.py:22
  341.2 0.0 reduce-scatter.17.cloned.1.call-start
  341.3 23.0 %fusion.30 = bf16[1664,512]{1,0:T(8,128)(2,1)} fusion(bf16[1,4096,512]{2,1,0:T(8,128)(2,1)} %param.12, f32[4096,1664]{1,0:T(8,128)} %fusion.39, f32[4096,1664]{1,0:T(8,128)} %get-tuple-element.29), kind=kOutput, calls=%fused_computation.50 | convolution fusion | flops 7021068288 | bytes 60424192 | tf_op jit(solution)/shard_map/transpose(jvp())/dot_general | solution.py:10
  364.3 0.0 reduce-scatter.15.cloned.1.call-start
  364.4 14.1 %convolution_convert_fusion.5 = bf16[1664,512]{1,0:T(8,128)(2,1)} fusion(bf16[4096,1664]{1,0:T(8,128)(2,1)} %get-tuple-element.24, bf16[4096,512]{0,1:T(8,128)(2,1)} %copy-done.3), kind=kOutput, calls=%fused_computation.52 | convolution fusion | flops 6980173824 | bytes 19529728 | tf_op jit(solution)/shard_map/transpose(jvp())/dot_general | solution.py:10
  378.6 2.6 fusion.60
  381.2 24.2 %reduce-scatter.11.cloned.1.call-done = bf16[64,1664]{1,0:T(8,128)(2,1)} async-done(((bf16[512,1664]{1,0:T(8,128)(2,1)}), bf16[64,1664]{1,0:T(8,128)(2,1)}) %reduce-scatter.11.cloned.1.call-update) | async-done | bytes 213008 | tf_op jit(solution)/shard_map/reduce_scatter | solution.py:48
  405.4 3.2 fusion.64
  408.6 32.0 %reduce-scatter.17.cloned.1.call-done = bf16[208,512]{1,0:T(8,128)(2,1)} async-done(((bf16[1664,512]{1,0:T(8,128)(2,1)}), bf16[208,512]{1,0:T(8,128)(2,1)}) %reduce-scatter.17.cloned.1.call-update) | async-done | bytes 213008 | tf_op jit(solution)/shard_map/reduce_scatter | solution.py:48
  440.6 35.0 %reduce-scatter.15.cloned.1.call-done = bf16[208,512]{1,0:T(8,128)(2,1)} async-done(((bf16[1664,512]{1,0:T(8,128)(2,1)}), bf16[208,512]{1,0:T(8,128)(2,1)}) %reduce-scatter.15.cloned.1.call-update) | async-done | bytes 213008 | tf_op jit(solution)/shard_map/reduce_scatter | solution.py:48
  475.6 3.2 fusion.68
  (46 shorter events, 0.3 us)
Async XLA Ops:
  7.2 31.9 %all-gather.13.cloned.1.call-start = ((), (), s32[]{:S(2)}) async-start(), calls=%async_computation.12 | async-start | bytes 1916928 | tf_op jit(solution)/shard_map/all_gather | solution.py:35
  9.1 57.6 %all-gather.15.cloned.1.call-start = ((), (), s32[]{:S(2)}) async-start(), calls=%async_computation.13 | async-start | bytes 1916928 | tf_op jit(solution)/shard_map/all_gather | solution.py:35
  11.0 83.4 %all-gather.17.cloned.1.call-start = ((), (), s32[]{:S(2)}) async-start(), calls=%async_computation.14 | async-start | bytes 1916928 | tf_op jit(solution)/shard_map/all_gather | solution.py:35
  12.9 108.8 %all-gather.21.cloned.1.call-start = ((), (), s32[]{:S(2)}) async-start(), calls=%async_computation.16 | async-start | bytes 1916928 | tf_op jit(solution)/shard_map/all_gather | solution.py:35
  13.4 135.6 %all-gather.23.cloned.1.call-start = ((), (), s32[]{:S(2)}) async-start(), calls=%async_computation.17 | async-start | bytes 1916928 | tf_op jit(solution)/shard_map/all_gather | solution.py:35
  14.0 162.4 %all-gather.19.cloned.1.call-start = ((), (), s32[]{:S(2)}) async-start(), calls=%async_computation.15 | async-start | bytes 1916928 | tf_op jit(solution)/shard_map/all_gather | solution.py:35
  14.6 364.0 %reduce-scatter.9.cloned.1.call-start = ((), (), s32[]{:S(2)}) async-start(), calls=%async_computation.7 | async-start | bytes 1916928 | tf_op jit(solution)/shard_map/reduce_scatter | solution.py:48
  24.2 42.5 %copy-start.11 = (f32[4096]{0:T(1024)}, f32[4096]{0:T(1024)S(1)}, u32[]{:S(2)}) copy-start(f32[4096]{0:T(1024)S(1)} %add_rsqrt_fusion) | copy-start | bytes 49156
  108.6 0.6 copy-start.9
  213.3 14.6 %copy-start.14 = (bf16[1,512,1664]{2,1,0:T(8,128)(2,1)S(1)}, bf16[1,512,1664]{2,1,0:T(8,128)(2,1)}, u32[]{:S(2)}) copy-start(bf16[1,512,1664]{2,1,0:T(8,128)(2,1)} %all-gather.23.cloned.1.call-done) | copy-start | bytes 5111812
  227.8 150.8 %reduce-scatter.7.cloned.1.call-start = ((), (), s32[]{:S(2)}) async-start(), calls=%async_computation.6 | async-start | bytes 1916928 | tf_op jit(solution)/shard_map/reduce_scatter | solution.py:48
  247.2 13.7 %copy-start.10 = (f32[4096]{0:T(1024)S(1)}, f32[4096]{0:T(1024)}, u32[]{:S(2)}) copy-start(f32[4096]{0:T(1024)} %copy-done.9) | copy-start | bytes 49156
  247.2 13.8 %copy-start.1 = (bf16[1,4096,512]{1,2,0:T(8,128)(2,1)S(1)}, bf16[1,4096,512]{1,2,0:T(8,128)(2,1)}, u32[]{:S(2)}) copy-start(bf16[1,4096,512]{1,2,0:T(8,128)(2,1)} %copy.21) | copy-start | bytes 12582916
  247.2 13.8 %copy-start.2 = (bf16[4096,512]{0,1:T(8,128)(2,1)S(1)}, bf16[4096,512]{0,1:T(8,128)(2,1)}, u32[]{:S(2)}) copy-start(bf16[4096,512]{0,1:T(8,128)(2,1)} %get-tuple-element.27) | copy-start | bytes 12582916
  261.0 3.2 copy-start.13
  264.1 11.2 %copy-start.3 = (bf16[4096,512]{0,1:T(8,128)(2,1)}, bf16[4096,512]{0,1:T(8,128)(2,1)S(1)}, u32[]{:S(2)}) copy-start(bf16[4096,512]{0,1:T(8,128)(2,1)S(1)} %fusion.26) | copy-start | bytes 12582916
  264.2 11.2 %copy-start = (bf16[1,4096,512]{1,2,0:T(8,128)(2,1)S(1)}, bf16[1,4096,512]{1,2,0:T(8,128)(2,1)}, u32[]{:S(2)}) copy-start(bf16[1,4096,512]{1,2,0:T(8,128)(2,1)} %copy.20) | copy-start | bytes 12582916
  264.2 11.2 %copy-start.12 = (f32[4096]{0:T(1024)S(1)}, f32[4096]{0:T(1024)}, u32[]{:S(2)}) copy-start(f32[4096]{0:T(1024)} %copy-done.11) | copy-start | bytes 49156
  301.1 80.1 %reduce-scatter.13.cloned.1.call-start = ((), (), s32[]{:S(2)}) async-start(), calls=%async_computation.9 | async-start | bytes 1916928 | tf_op jit(solution)/shard_map/reduce_scatter | solution.py:48
  321.4 84.0 %reduce-scatter.11.cloned.1.call-start = ((), (), s32[]{:S(2)}) async-start(), calls=%async_computation.8 | async-start | bytes 1916928 | tf_op jit(solution)/shard_map/reduce_scatter | solution.py:48
  341.2 99.3 %reduce-scatter.17.cloned.1.call-start = ((), (), s32[]{:S(2)}) async-start(), calls=%async_computation.11 | async-start | bytes 1916928 | tf_op jit(solution)/shard_map/reduce_scatter | solution.py:48
  364.3 14.3 %copy-start.4 = (bf16[2,64,1664]{2,1,0:T(8,128)(2,1)S(1)}, bf16[2,64,1664]{2,1,0:T(8,128)(2,1)}, u32[]{:S(2)}) copy-start(bf16[2,64,1664]{2,1,0:T(8,128)(2,1)} %param.13) | copy-start | bytes 1277956
  364.3 14.3 %copy-start.7 = (f32[2,64,1664]{2,1,0:T(8,128)S(1)}, f32[2,64,1664]{2,1,0:T(8,128)}, u32[]{:S(2)}) copy-start(f32[2,64,1664]{2,1,0:T(8,128)} %param.19) | copy-start | bytes 2555908
  364.3 14.3 %copy-start.8 = (f32[2,64,1664]{2,1,0:T(8,128)S(1)}, f32[2,64,1664]{2,1,0:T(8,128)}, u32[]{:S(2)}) copy-start(f32[2,64,1664]{2,1,0:T(8,128)} %param.16) | copy-start | bytes 2555908
  364.3 41.1 %copy-start.5 = (bf16[2,64,1664]{2,1,0:T(8,128)(2,1)S(1)}, bf16[2,64,1664]{2,1,0:T(8,128)(2,1)}, u32[]{:S(2)}) copy-start(bf16[2,64,1664]{2,1,0:T(8,128)(2,1)} %param.14) | copy-start | bytes 1277956
  364.3 111.3 %reduce-scatter.15.cloned.1.call-start = ((), (), s32[]{:S(2)}) async-start(), calls=%async_computation.10 | async-start | bytes 1916928 | tf_op jit(solution)/shard_map/reduce_scatter | solution.py:48
  378.5 97.1 %copy-start.6 = (bf16[2,208,512]{2,1,0:T(8,128)(2,1)S(1)}, bf16[2,208,512]{2,1,0:T(8,128)(2,1)}, u32[]{:S(2)}) copy-start(bf16[2,208,512]{2,1,0:T(8,128)(2,1)} %param.15) | copy-start | bytes 1277956
Sparse Core Ops, SparseCore 0:
  10.2 28.8 all-gather.12
  41.3 25.2 all-gather.14
  68.9 25.2 all-gather.16
  96.3 25.3 all-gather.20
  123.7 25.2 all-gather.22
  151.1 25.2 all-gather.18
  227.9 33.8 reduce-scatter.8
  301.2 33.8 reduce-scatter.6
  337.5 32.8 reduce-scatter.12
  372.5 32.8 reduce-scatter.10
  407.7 32.8 reduce-scatter.16
  442.7 32.8 reduce-scatter.14
where the time goes:
time: 494 us; the launch traced here: 486 us
  matrix products  283 us (57%)
  waiting for transfers between devices  153 us (31%)
  local copies, waits for them, and re-layouts  19.1 us (4%)
  other arithmetic  15.2 us (3%)
  between operations  14.9 us (3%)
    dot_general x5, matrix products, layer(): gate = jnp.dot(a, w['w_gate'], preferred_element_type=jnp.float32)  106 us
    dot_general x5, matrix products, layer(): up = jnp.dot(a, w['w_up'], preferred_element_type=jnp.float32)  102 us
    reduce_scatter x6, waiting for transfers between devices, step(): lax.psum_scatter(by_w[name], 'dp', scatter_dimension=0, tiled=True)  91.3 us
    dot_general x5, matrix products, matmul(): jnp.dot(a, w, preferred_element_type=jnp.float32).astype(jnp.bfloat16)  75.4 us
    all_gather x6, waiting for transfers between devices, fetched(): lax.all_gather(w[number], 'dp', axis=0, tiled=True)  60.2 us
    unnamed x32, local copies, waits for them, and re-layouts  13.6 us
  transfers between devices with their start and end apart: 12, of which 8 were waited for; matrix products, arithmetic and copies ran while one was open for 54% of the time, Pallas kernels for 0%

commit v1 on v0

v1 whole, which is shorter than its diff:
```python
import functools

import jax
import jax.numpy as jnp
from jax import lax
from jax.experimental import pallas as pl
from jax.experimental.pallas import tpu as pltpu
from jax.sharding import PartitionSpec as P

T, D, FF = 4096, 512, 1664
UNITS = 13
GROUPS = 7
TILE = 512
TILES = T // TILE
VMEM_LIMIT = 67_043_328
BF, F32 = jnp.bfloat16, jnp.float32
BLOCKS = (UNITS, 2, 2, 2, 96, 256)


def dot(a, b):
    return lax.dot_general(a, b, (((1,), (0,)), ((), ())), preferred_element_type=F32)


def dot_nt(a, b):
    return lax.dot_general(a, b, (((1,), (1,)), ((), ())), preferred_element_type=F32)


def rms(h):
    wide = h.astype(F32)
    return wide, lax.rsqrt(jnp.mean(wide * wide, -1, keepdims=True) + 1e-6)


def place():
    me = lax.axis_index("dp")
    z1, z0, c = lax.div(me, 4), lax.rem(lax.div(me, 2), 2), lax.rem(me, 2)
    return z1, z0, c, (me + 1 - 2 * c, me + 2 - 4 * z0, me + 4 - 8 * z1)


def greet(partners):
    barrier = pltpu.get_barrier_semaphore()
    for p in partners:
        pl.semaphore_signal(barrier, inc=1, device_id={"dp": p}, device_id_type=pl.DeviceIdType.MESH)
    pl.semaphore_wait(barrier, 3)


def gather_copy(stage, u, w, send, recv, at):
    z1, z0, c, partners = at
    ref = (w.at[u, z1, z0, c], w.at[u, :, z0, c], w.at[u, :, :, c])[stage]
    return pltpu.make_async_remote_copy(
        src_ref=ref,
        dst_ref=ref,
        send_sem=send.at[stage, u],
        recv_sem=recv.at[stage, u],
        device_id={"dp": partners[2 - stage]},
        device_id_type=pl.DeviceIdType.MESH,
    )


def gather_tick(i, w, send, recv, at):
    @pl.when(i < UNITS)
    def _():
        gather_copy(0, i, w, send, recv, at).start()

    @pl.when((i >= 2) & (i < UNITS + 2))
    def _():
        gather_copy(0, i - 2, w, send, recv, at).wait_recv()
        gather_copy(1, i - 2, w, send, recv, at).start()

    @pl.when((i >= 4) & (i < UNITS + 4))
    def _():
        gather_copy(1, i - 4, w, send, recv, at).wait_recv()
        gather_copy(2, i - 4, w, send, recv, at).start()


def gather_ready(u, w, send, recv, at):
    gather_copy(2, u, w, send, recv, at).wait_recv()


def gather_end(w, send, recv, at):
    def one(u, carry):
        for stage in range(3):
            gather_copy(stage, u, w, send, recv, at).wait_send()
        return carry

    lax.fori_loop(0, UNITS, one, 0)


def scatter_copy(stage, s, n, bufs, send, recv, at):
    z1, z0, c, partners = at
    own, r1, r2, r3 = bufs
    u = pl.ds(2 * s, n)
    src = (own.at[u, :, :, 1 - c], r1.at[u, :, 1 - z0], r2.at[u, 1 - z1])[stage]
    dst = (r1, r2, r3)[stage].at[u]
    return pltpu.make_async_remote_copy(
        src_ref=src,
        dst_ref=dst,
        send_sem=send.at[stage, s],
        recv_sem=recv.at[stage, s],
        device_id={"dp": partners[stage]},
        device_id_type=pl.DeviceIdType.MESH,
    )


def scatter_advance(stage, s, n, bufs, g_ref, send, recv, at):
    z1, z0, c, partners = at
    own, r1, r2, r3 = bufs
    scatter_copy(stage, s, n, bufs, send, recv, at).wait_recv()
    for j in range(n):
        u = 2 * s + j
        if stage == 0:
            r1[u] = (r1[u].astype(F32) + own[u, :, :, c].astype(F32)).astype(BF)
        elif stage == 1:
            r2[u] = (r2[u].astype(F32) + r1[u, :, z0].astype(F32)).astype(BF)
        else:
            g_ref[u] = (r3[u].astype(F32) + r2[u, z1].astype(F32)).astype(BF)
    if stage < 2:
        scatter_copy(stage + 1, s, n, bufs, send, recv, at).start()


def scatter_end(bufs, send, recv, at):
    for stage in range(3):

        def one(s, carry, stage=stage):
            scatter_copy(stage, s, 2, bufs, send, recv, at).wait_send()
            return carry

        lax.fori_loop(0, GROUPS - 1, one, 0)
        scatter_copy(stage, GROUPS - 1, 1, bufs, send, recv, at).wait_send()


def tile_rows(t):
    return pl.ds(pl.multiple_of(t * TILE, TILE), TILE)


def forward_kernel(x_ref, own_ref, h_ref, w_out, a_ref, act_ref, w, send, recv, sem):
    at = place()
    z1, z0, c, partners = at
    bring = pltpu.make_async_copy(own_ref, w.at[:, z1, z0, c], sem.at[0])
    bring.start()
    greet(partners)
    bring.wait()
    for i in range(3):
        gather_tick(i, w, send, recv, at)

    def norm(t, carry):
        rows = tile_rows(t)
        wide, scale = rms(x_ref[rows, :])
        a_ref[rows, :] = (wide * scale).astype(BF)
        return carry

    lax.fori_loop(0, TILES, norm, 0)
    for i in range(3, 5):
        gather_tick(i, w, send, recv, at)

    def unit(u, carry):
        gather_tick(u + 5, w, send, recv, at)
        gather_ready(u, w, send, recv, at)
        columns = pl.ds(pl.multiple_of(u * 128, 128), 128)
        w_gu = w[u, :, :, :, :64, :].reshape(D, 256)

        def tile(t, carry):
            rows = tile_rows(t)
            gu = dot(a_ref[rows, :], w_gu)
            act_ref[rows, columns] = (jax.nn.silu(gu[:, :128]) * gu[:, 128:]).astype(BF)
            return carry

        return lax.fori_loop(0, TILES, tile, carry)

    lax.fori_loop(0, UNITS, unit, 0)
    save = pltpu.make_async_copy(w, w_out, sem.at[1])
    save.start()

    def down(t, carry):
        rows = tile_rows(t)
        act = act_ref[rows, :]
        for half in range(2):
            w_d = w[:, :, :, :, 64 + 16 * half : 80 + 16 * half, :].reshape(FF, 256)
            columns = slice(256 * half, 256 * half + 256)
            h_ref[rows, columns] = x_ref[rows, columns] + dot(act, w_d).astype(BF)
        return carry

    lax.fori_loop(0, TILES, down, 0)
    gather_end(w, send, recv, at)
    save.wait()


def backward_group(s, n, first, refs):
    a_ref, a_t, dy_ref, dy_t, da_ref, w, dgu_ref, act_ref, own = refs

    def tile(t, carry):
        rows = tile_rows(t)
        a, dy = a_ref[rows, :], dy_ref[rows, :]
        w_d = [w[pl.ds(2 * s, n), :, :, :, 64 + 16 * h : 80 + 16 * h, :].reshape(n * 128, 256) for h in range(2)]
        dact = dot_nt(dy[:, :256], w_d[0]) + dot_nt(dy[:, 256:], w_d[1])
        dact = dact.astype(BF).astype(F32)
        da = None
        for j in range(n):
            w_gu = w[2 * s + j, :, :, :, :64, :].reshape(D, 256)
            gu = dot(a, w_gu)
            gate, up = gu[:, :128], gu[:, 128:]
            sig = jax.nn.sigmoid(gate)
            silu = gate * sig
            act_ref[rows, 128 * j : 128 * j + 128] = (silu * up).astype(BF)
            mine = dact[:, 128 * j : 128 * j + 128]
            dgate = mine * up * (sig + silu * (1 - sig))
            dgu = jnp.concatenate([dgate.astype(BF), (mine * silu).astype(BF)], axis=1)
            dgu_ref[j, rows, :] = dgu
            if not first:
                term = dot_nt(dgu, w_gu)
                da = term if da is None else da + term
        if not first:
            da_ref[rows, :] += da
        return carry

    lax.fori_loop(0, TILES, tile, 0)
    for j in range(n):
        by_gu = dot(a_t[...], dgu_ref[j]).astype(BF)
        own[2 * s + j, :, :, :, :64, :] = by_gu.reshape(2, 2, 2, 64, 256)
    by_d = dot(dy_t[...], act_ref[:, : 128 * n])
    for j in range(n):
        for h in range(2):
            piece = by_d[256 * h : 256 * h + 256, 128 * j : 128 * j + 128].T.astype(BF)
            own[2 * s + j, :, :, :, 64 + 16 * h : 80 + 16 * h, :] = piece.reshape(2, 2, 2, 16, 256)


def backward_all(first, refs, bufs, g_ref, send, recv, at, before):
    def advance(s):
        for stage in range(3):

            @pl.when(s >= stage + 1)
            def _(stage=stage):
                scatter_advance(stage, s - 1 - stage, 2, bufs, g_ref, send, recv, at)

    def group(s, carry):
        before(s, 2)
        backward_group(s, 2, first, refs)
        advance(s)
        scatter_copy(0, s, 2, bufs, send, recv, at).start()
        return carry

    last = GROUPS - 1
    lax.fori_loop(0, last, group, 0)
    before(last, 1)
    backward_group(last, 1, first, refs)
    for stage in range(3):
        scatter_advance(stage, last - 1 - stage, 2, bufs, g_ref, send, recv, at)
    scatter_copy(0, last, 1, bufs, send, recv, at).start()


def backward_drain(bufs, g_ref, send, recv, at):
    last = GROUPS - 1
    scatter_advance(0, last, 1, bufs, g_ref, send, recv, at)
    scatter_advance(1, last - 1, 2, bufs, g_ref, send, recv, at)
    scatter_advance(2, last - 2, 2, bufs, g_ref, send, recv, at)
    scatter_advance(1, last, 1, bufs, g_ref, send, recv, at)
    scatter_advance(2, last - 1, 2, bufs, g_ref, send, recv, at)
    scatter_advance(2, last, 1, bufs, g_ref, send, recv, at)
    scatter_end(bufs, send, recv, at)


def set_out(h_ref, dy_ref, a_ref, a_t, dy_t, da_ref):
    def one(t, carry):
        rows = tile_rows(t)
        wide, scale = rms(h_ref[rows, :])
        a = (wide * scale).astype(BF)
        a_ref[rows, :] = a
        a_t[:, rows] = a.T
        dy_t[:, rows] = dy_ref[rows, :].T
        if da_ref is not None:
            da_ref[rows, :] = jnp.zeros((TILE, D), F32)
        return carry

    lax.fori_loop(0, TILES, one, 0)


def last_layer_kernel(
    h_ref, dy_ref, own_w, dh_ref, g_ref, a_ref, a_t, dy_t, da_ref, w, dgu_ref, act_ref, own, r1, r2, r3, wsend, wrecv, send, recv, sem
):
    at = place()
    z1, z0, c, partners = at
    bring = pltpu.make_async_copy(own_w, w.at[:, z1, z0, c], sem.at[0])
    bring.start()
    greet(partners)
    bring.wait()
    for i in range(3):
        gather_tick(i, w, wsend, wrecv, at)
    set_out(h_ref, dy_ref, a_ref, a_t, dy_t, da_ref)
    for i in range(3, 5):
        gather_tick(i, w, wsend, wrecv, at)

    def before(s, n):
        for j in range(n):
            gather_tick(2 * s + j + 5, w, wsend, wrecv, at)
        for j in range(n):
            gather_ready(2 * s + j, w, wsend, wrecv, at)

    bufs = (own, r1, r2, r3)
    backward_all(False, (a_ref, a_t, dy_ref, dy_t, da_ref, w, dgu_ref, act_ref, own), bufs, g_ref, send, recv, at, before)

    def norm(t, carry):
        rows = tile_rows(t)
        wide, scale = rms(h_ref[rows, :])
        da = da_ref[rows, :].astype(BF).astype(F32)
        along = jnp.sum(da * wide, -1, keepdims=True) * (scale * scale * scale * (1.0 / D))
        by_h = (da * scale - wide * along).astype(BF)
        dh_ref[rows, :] = dy_ref[rows, :] + by_h
        return carry

    lax.fori_loop(0, TILES, norm, 0)
    gather_end(w, wsend, wrecv, at)
    backward_drain(bufs, g_ref, send, recv, at)


def first_layer_kernel(h_ref, dy_ref, w, g_ref, a_ref, a_t, dy_t, dgu_ref, act_ref, own, r1, r2, r3, send, recv):
    at = place()
    greet(at[3])
    set_out(h_ref, dy_ref, a_ref, a_t, dy_t, None)
    bufs = (own, r1, r2, r3)
    refs = (a_ref, a_t, dy_ref, dy_t, None, w, dgu_ref, act_ref, own)
    backward_all(True, refs, bufs, g_ref, send, recv, at, lambda s, n: None)
    backward_drain(bufs, g_ref, send, recv, at)


def vmem(*shape):
    return pltpu.VMEM(shape, BF)


IN_VMEM = pl.BlockSpec(memory_space=pltpu.VMEM)
ANYWHERE = pl.BlockSpec(memory_space=pl.ANY)
DMA = pltpu.SemaphoreType.DMA


def call(kernel, name, number, in_specs, out, out_specs, scratch, flops):
    return pl.pallas_call(
        kernel,
        name=name,
        out_shape=out,
        in_specs=in_specs,
        out_specs=out_specs,
        scratch_shapes=scratch,
        compiler_params=pltpu.CompilerParams(collective_id=number, has_side_effects=True, vmem_limit_bytes=VMEM_LIMIT),
        cost_estimate=pl.CostEstimate(flops=flops, bytes_accessed=20_000_000, transcendentals=0),
    )


def shape(*dims):
    return jax.ShapeDtypeStruct(dims, BF)


MATMUL = 2 * T * D * FF
SUMS = [
    vmem(*BLOCKS),
    vmem(UNITS, 2, 2, 96, 256),
    vmem(UNITS, 2, 96, 256),
    vmem(UNITS, 96, 256),
]


def forward(x, own):
    return call(
        forward_kernel,
        "forward",
        0,
        [IN_VMEM, ANYWHERE],
        (shape(T, D), shape(*BLOCKS)),
        (IN_VMEM, ANYWHERE),
        [vmem(T, D), vmem(T, FF), vmem(*BLOCKS), DMA((3, UNITS)), DMA((3, UNITS)), DMA((2,))],
        3 * MATMUL,
    )(x, own)


def last_layer(h, dy, own):
    return call(
        last_layer_kernel,
        "last_layer",
        1,
        [IN_VMEM, IN_VMEM, ANYWHERE],
        (shape(T, D), shape(UNITS, 96, 256)),
        (IN_VMEM, IN_VMEM),
        [
            vmem(T, D),
            vmem(D, T),
            vmem(D, T),
            pltpu.VMEM((T, D), F32),
            vmem(*BLOCKS),
            vmem(2, T, 256),
            vmem(T, 256),
            *SUMS,
            DMA((3, UNITS)),
            DMA((3, UNITS)),
            DMA((3, GROUPS)),
            DMA((3, GROUPS)),
            DMA((1,)),
        ],
        8 * MATMUL,
    )(h, dy, own)


def first_layer(x, dh, w):
    return call(
        first_layer_kernel,
        "first_layer",
        2,
        [IN_VMEM, IN_VMEM, IN_VMEM],
        shape(UNITS, 96, 256),
        IN_VMEM,
        [vmem(T, D), vmem(D, T), vmem(D, T), vmem(2, T, 256), vmem(T, 256), *SUMS, DMA((3, GROUPS)), DMA((3, GROUPS))],
        6 * MATMUL,
    )(x, dh, w)


def to_units(w_gate, w_up, w_down):
    layers = w_gate.shape[0]
    wide = [w.reshape(layers, 64, 8, UNITS, 16).transpose(0, 3, 1, 2, 4).reshape(layers, UNITS, 64, 128) for w in (w_gate, w_up)]
    down = w_down.reshape(layers, UNITS, 16, 2, 256).transpose(0, 1, 3, 2, 4).reshape(layers, UNITS, 32, 256)
    return jnp.concatenate([jnp.concatenate(wide, -1), down], 2)


def from_units(g):
    layers = g.shape[0]
    wide = [
        g[:, :, :64, at : at + 128].reshape(layers, UNITS, 64, 8, 16).transpose(0, 2, 3, 1, 4).reshape(layers, 64, FF) for at in (0, 128)
    ]
    down = g[:, :, 64:].reshape(layers, UNITS, 2, 16, 256).transpose(0, 1, 3, 2, 4).reshape(layers, 208, D)
    return *wide, down


def adamw(w, m, v, g):
    m = 0.9 * m + 0.1 * g
    v = 0.95 * v + 0.05 * g * g
    step = m * lax.rsqrt(v + 1e-8) + 0.1 * w
    return (w - 0.02 * step).astype(BF), m, v


def solution(mesh):
    def step(x, dy, *arrays):
        weights, m, v = (arrays[i : i + 3] for i in (0, 3, 6))
        own = to_units(*weights)
        h, w0 = forward(x[0], own[0])
        dh, g1 = last_layer(h, dy[0], own[1])
        g0 = first_layer(x[0], dh, w0)
        gradients = from_units(jnp.stack([g0, g1]))
        new = [adamw(w.astype(F32), m, v, g.astype(F32)) for w, m, v, g in zip(weights, m, v, gradients, strict=True)]
        return tuple(one[which] for which in range(3) for one in new)

    states, cut = P(("rep", "dp"), None, None), P(None, "dp", None)
    return jax.shard_map(
        step,
        mesh=mesh,
        in_specs=(states, states) + (cut,) * 9,
        out_specs=(P("rep", "dp", None),) * 9,
        check_vma=False,
    )
```

time: 494 us -> 324 us (0.66); the launches traced: 486 us -> 323 us
  Pallas kernels: 0 us -> 302 us
  matrix products: 283 us -> 0 us
  waiting for transfers between devices: 153 us -> 0 us
  between operations: 14.9 us -> 0.84 us
  local copies, waits for them, and re-layouts: 19.1 us -> 10.8 us
  other arithmetic: 15.2 us -> 9.97 us
    pallas_call x0 -> x3, Pallas kernels: none -> 302 us  [the longest x1 146 us: last_layer(): call(last_layer_kernel, 'last_layer', 1, [IN_VMEM, IN_VMEM, ANYWHERE], (s...]
    dot_general x15 -> x0, matrix products: 283 us -> none  [the longest x5 106 us: layer(): gate = jnp.dot(a, w['w_gate'], preferred_element_type=jnp.float32)]
    reduce_scatter x6 -> x0, waiting for transfers between devices: 91.3 us -> none  [step(): lax.psum_scatter(by_w[name], 'dp', scatter_dimension=0, tiled=True)]
    all_gather x6 -> x0, waiting for transfers between devices: 60.2 us -> none  [fetched(): lax.all_gather(w[number], 'dp', axis=0, tiled=True)]
    unnamed x32 -> x18, local copies, waits for them, and re-layouts: 13.6 us -> 1.94 us
    slice x3 -> x0, local copies, waits for them, and re-layouts: 5.46 us -> none  [fetched(): w[number]]
    convert_element_type x0 -> x8, local copies, waits for them, and re-layouts: none -> 5.36 us  [step(): g.astype(F32)]
  transfers between devices with their start and end apart: 12 -> 0, of which waited for: 8 -> 0; matrix products, arithmetic and copies ran while one was open for 54% -> 0% of each run, Pallas kernels for 0% -> 0%
where the time goes in v1:
time: 324 us; the launch traced here: 323 us
  Pallas kernels  302 us (93%)
  local copies, waits for them, and re-layouts  10.8 us (3%)
  other arithmetic  9.97 us (3%)
    pallas_call x1, Pallas kernels, last_layer(): call(last_layer_kernel, 'last_layer', 1, [IN_VMEM, IN_VMEM, ANYWHERE], (s...  146 us
    pallas_call x1, Pallas kernels, first_layer(): call(first_layer_kernel, 'first_layer', 2, [IN_VMEM, IN_VMEM, IN_VMEM], s...  84.6 us
    pallas_call x1, Pallas kernels, forward(): call(forward_kernel, 'forward', 0, [IN_VMEM, ANYWHERE], (shape(T, D), sha...  70.7 us
    convert_element_type x2, other arithmetic, adamw(): return ((w - 0.02 * step).astype(BF), m, v)  7.65 us

profile of v1, /device:TPU:0, one launch (start us, length us, event | category | flops | bytes accessed | tf_op | source)
XLA Modules:
  0.0 323.2 jit_solution(14398407064065456725)
XLA Ops:
  0.6 0.0 copy-start.6
  0.7 1.2 reshape.58
  1.8 0.1 copy.56
  1.9 0.0 copy-done.6
  1.9 0.4 copy.50
  2.3 0.0 copy-start.7
  2.3 0.2 copy.51
  2.5 0.3 copy.54
  2.9 0.4 copy-done.7
  3.3 0.4 copy.52
  3.7 0.2 copy.53
  4.0 0.3 copy.55
  4.3 0.1 pad_maximum_fusion
  4.5 1.1 slice_bitcast_fusion
  5.6 70.7 %forward.1 = (bf16[4096,512]{1,0:T(8,128)(2,1)}, bf16[13,2,2,2,96,256]{5,4,3,2,1,0:T(8,128)(2,1)}) custom-call(bf16[4096,512]{1,0:T(8,128)(2,1)} %bitcast.46, bf16[13,96,256]{2,1,0:T(8,128)(2,1)} %get-tuple-element.38.own_ref), custom_call_target="tpu_custom_call" | custom-call | flops 20937965568 | bytes 20000000 | tf_op jit(solution)/shard_map/forward/pallas_call | solution.py:360
  76.3 146.3 %last_layer.1 = (bf16[4096,512]{1,0:T(8,128)(2,1)}, bf16[13,96,256]{2,1,0:T(8,128)(2,1)}) custom-call(bf16[4096,512]{1,0:T(8,128)(2,1)} %get-tuple-element.13.h_ref, bf16[4096,512]{1,0:T(8,128)(2,1)} %bitcast.45, bf16[13,96,256]{2,1,0:T(8,128)(2,1)} %get-tuple-element.37.own_w), custom_call_target="tpu_custom_call" | custom-call | flops 55834574848 | bytes 20000000 | tf_op jit(solution)/shard_map/last_layer/pallas_call | solution.py:373
  222.6 84.6 %first_layer.1 = bf16[13,96,256]{2,1,0:T(8,128)(2,1)} custom-call(bf16[4096,512]{1,0:T(8,128)(2,1)} %bitcast.47, bf16[4096,512]{1,0:T(8,128)(2,1)} %get-tuple-element.14.dy_ref, bf16[13,2,2,2,96,256]{5,4,3,2,1,0:T(8,128)(2,1)} %get-tuple-element.15.w), custom_call_target="tpu_custom_call" | custom-call | flops 41875931136 | bytes 20000000 | tf_op jit(solution)/shard_map/first_layer/pallas_call | solution.py:400
  307.3 1.1 pad_maximum_fusion.1
  308.3 0.1 convert_bitcast_fusion
  308.4 0.0 copy-start.3
  308.4 0.0 copy-start.4
  308.5 0.7 copy.67
  309.1 1.6 reshape.62
  310.7 0.0 copy-done.3
  310.7 0.0 copy-done.4
  310.7 1.0 fusion.13
  311.7 0.5 copy.62
  312.2 0.1 copy.63
  312.4 0.0 copy-start.1
  312.4 0.0 copy-start.5
  312.4 1.4 copy.64
  313.8 0.0 copy-done.1
  313.8 0.0 copy-done.5
  313.8 0.0 copy-start.2
  313.8 3.1 fusion.8
  316.9 0.0 copy-done.2
  316.9 0.5 copy.57
  317.4 0.1 copy.58
  317.5 0.0 copy-start
  317.5 0.5 copy.59
  318.0 0.7 copy-done
  318.7 4.6 %fusion.2 = (bf16[2,64,1664]{2,1,0:T(8,128)(2,1)}, f32[2,64,1664]{2,1,0:T(8,128)}, f32[2,64,1664]{2,1,0:T(8,128)}, bf16[2,64,1664]{2,1,0:T(8,128)(2,1)}, f32[2,64,1664]{2,1,0:T(8,128)}, /*index=5*/f32[2,64,1664]{2,1,0:T(8,128)}) fusion(bf16[2,64,1664]{2,1,0:T(8,128)(2,1)} %param.13, f32[2,64,1664]{2,1,0:T(8,128)S(1)} %copy.59, f32[2,64,1664]{2,1,0:T(8,128)} %param.19, ...), kind=kLoop, calls=%fused_computation.16 | loop fusion | flops 6389760 | bytes 10223616 | tf_op jit(solution)/shard_map/convert_element_type | solution.py:432
Async XLA Ops:
  0.6 1.2 copy-start.6
  2.3 1.0 copy-start.7
  308.4 2.3 copy-start.3
  308.4 2.3 copy-start.4
  312.4 1.4 copy-start.1
  312.4 1.4 copy-start.5
  313.8 3.1 copy-start.2
  317.5 1.2 copy-start

commit v2 on v0

v2 whole, which is shorter than its diff:
```python
import functools

import jax
import jax.numpy as jnp
from jax import lax
from jax.experimental import pallas as pl
from jax.experimental.pallas import tpu as pltpu
from jax.sharding import PartitionSpec as P

T, D, FF = 4096, 512, 1664
UNITS = 13
GROUPS = 7
TILE = 512
VMEM_LIMIT = 67_043_328
BF, F32 = jnp.bfloat16, jnp.float32
BOTH = 2 * UNITS


def dot(a, b):
    return lax.dot_general(a, b, (((1,), (0,)), ((), ())), preferred_element_type=F32)


def dot_nt(a, b):
    return lax.dot_general(a, b, (((1,), (1,)), ((), ())), preferred_element_type=F32)


def rms(h):
    wide = h.astype(F32)
    return wide, lax.rsqrt(jnp.mean(wide * wide, -1, keepdims=True) + 1e-6)


def place():
    me = lax.axis_index("dp")
    z1, z0, c = lax.div(me, 4), lax.rem(lax.div(me, 2), 2), lax.rem(me, 2)
    return z1, z0, c, (me + 1 - 2 * c, me + 2 - 4 * z0, me + 4 - 8 * z1)


def greet(partners):
    barrier = pltpu.get_barrier_semaphore()
    for p in partners:
        pl.semaphore_signal(barrier, inc=1, device_id={"dp": p}, device_id_type=pl.DeviceIdType.MESH)
    pl.semaphore_wait(barrier, 3)


def gather_copy(stage, u, w, send, recv, at):
    z1, z0, c, partners = at
    ref = (w.at[u, z1, z0, c], w.at[u, :, z0, c], w.at[u, :, :, c])[stage]
    return pltpu.make_async_remote_copy(
        src_ref=ref,
        dst_ref=ref,
        send_sem=send.at[stage, u],
        recv_sem=recv.at[stage, u],
        device_id={"dp": partners[2 - stage]},
        device_id_type=pl.DeviceIdType.MESH,
    )


def gather_tick(i, w, send, recv, at):
    @pl.when(i < BOTH)
    def _():
        gather_copy(0, i, w, send, recv, at).start()

    @pl.when((i >= 2) & (i < BOTH + 2))
    def _():
        gather_copy(0, i - 2, w, send, recv, at).wait_recv()
        gather_copy(1, i - 2, w, send, recv, at).start()

    @pl.when((i >= 4) & (i < BOTH + 4))
    def _():
        gather_copy(1, i - 4, w, send, recv, at).wait_recv()
        gather_copy(2, i - 4, w, send, recv, at).start()


def gather_ready(u, w, send, recv, at):
    gather_copy(2, u, w, send, recv, at).wait_recv()


def gather_sent(u, w, send, recv, at):
    for stage in range(3):
        gather_copy(stage, u, w, send, recv, at).wait_send()


def scatter_copy(stage, u, n, bufs, send, recv, at):
    z1, z0, c, partners = at
    own, r1, r2, r3 = bufs
    us = pl.ds(u, n)
    src = (own.at[us, :, :, 1 - c], r1.at[us, :, 1 - z0], r2.at[us, 1 - z1])[stage]
    dst = (r1, r2, r3)[stage].at[us]
    return pltpu.make_async_remote_copy(
        src_ref=src,
        dst_ref=dst,
        send_sem=send.at[stage, u],
        recv_sem=recv.at[stage, u],
        device_id={"dp": partners[stage]},
        device_id_type=pl.DeviceIdType.MESH,
    )


def scatter_advance(stage, u, n, bufs, g_ref, send, recv, at):
    z1, z0, c, partners = at
    own, r1, r2, r3 = bufs
    scatter_copy(stage, u, n, bufs, send, recv, at).wait_recv()
    for v in range(n):
        v = u + v
        if stage == 0:
            r1[v] = (r1[v].astype(F32) + own[v, :, :, c].astype(F32)).astype(BF)
        elif stage == 1:
            r2[v] = (r2[v].astype(F32) + r1[v, :, z0].astype(F32)).astype(BF)
        else:
            g_ref[v] = (r3[v].astype(F32) + r2[v, z1].astype(F32)).astype(BF)
    if stage < 2:
        scatter_copy(stage + 1, u, n, bufs, send, recv, at).start()


def over(tile, body):
    def one(t, carry):
        body(pl.ds(pl.multiple_of(t * tile, tile), tile))
        return carry

    lax.fori_loop(0, T // tile, one, 0)


def groups(body):
    def one(s, carry):
        body(s, 2)
        return carry

    lax.fori_loop(0, GROUPS - 1, one, 0)
    body(GROUPS - 1, 1)


def w_gu_of(w, u):
    return w[u, :, :, :, :64, :].reshape(D, 256)


def w_d_of(w, u, n, half):
    return w[pl.ds(u, n), :, :, :, 64 + 16 * half : 80 + 16 * half, :].reshape(n * 128, 256)


def forward_group(u, n, a_ref, acc_ref, w):
    def tile(rows):
        a = a_ref[rows, :]
        act = []
        for j in range(n):
            gu = dot(a, w_gu_of(w, u + j))
            act.append((jax.nn.silu(gu[:, :128]) * gu[:, 128:]).astype(BF))
        act = jnp.concatenate(act, axis=1) if n > 1 else act[0]
        for half in range(2):
            columns = slice(256 * half, 256 * half + 256)
            acc_ref[rows, columns] += dot(act, w_d_of(w, u, n, half))

    over(TILE, tile)


def backward_group(u, n, first, refs, sent):
    a_ref, a_t, dy_ref, dy_t, da_ref, w, w_t, w_dt, dgu_ref, act_ref = refs
    for j in range(n):
        if not first:
            w_t[256 * j : 256 * j + 256, :] = w_gu_of(w, u + j).T
    for half in range(2):
        w_dt[256 * half : 256 * half + 256, : 128 * n] = w_d_of(w, u, n, half).T

    def tile(rows):
        a = a_ref[rows, :]
        dact = dot(dy_ref[rows, :], w_dt[:, : 128 * n]).astype(BF).astype(F32)
        for j in range(n):
            gu = dot(a, w_gu_of(w, u + j))
            gate, up = gu[:, :128], gu[:, 128:]
            sig = jax.nn.sigmoid(gate)
            silu = gate * sig
            mine = dact[:, 128 * j : 128 * j + 128]
            act_ref[rows, 128 * j : 128 * j + 128] = (silu * up).astype(BF)
            dgu_ref[rows, 256 * j : 256 * j + 128] = (mine * up * (sig + silu * (1 - sig))).astype(BF)
            dgu_ref[rows, 256 * j + 128 : 256 * j + 256] = (mine * silu).astype(BF)
        if not first:
            da_ref[rows, :] += dot(dgu_ref[rows, : 256 * n], w_t[: 256 * n, :])

    over(TILE, tile)
    for j in range(n):
        sent(u + j)
        by_gu = dot(a_t[...], dgu_ref[:, 256 * j : 256 * j + 256]).astype(BF)
        w[u + j, :, :, :, :64, :] = by_gu.reshape(2, 2, 2, 64, 256)
    by_d = dot(dy_t[...], act_ref[:, : 128 * n])
    for j in range(n):
        for h in range(2):
            piece = by_d[256 * h : 256 * h + 256, 128 * j : 128 * j + 128].T.astype(BF)
            w[u + j, :, :, :, 64 + 16 * h : 80 + 16 * h, :] = piece.reshape(2, 2, 2, 16, 256)


def normed(h):
    wide, scale = rms(h)
    return (wide * scale).astype(BF)


def kernel(
    x_ref, dy_in, own, g_ref, h_ref, a_ref, a_t, dy_ref, dy_t, acc_ref, w, w_t, w_dt, dgu_ref, act_ref, r1, r2, r3, gsend, grecv, ssend, srecv, sem
):
    at = place()
    z1, z0, c, partners = at
    halves = [pl.ds(0, UNITS), pl.ds(UNITS, UNITS)]
    bring = [pltpu.make_async_copy(own.at[us], w.at[us, z1, z0, c], sem.at[i]) for i, us in enumerate(halves)]
    bring += [pltpu.make_async_copy(x_ref, h_ref, sem.at[2]), pltpu.make_async_copy(dy_in, dy_ref, sem.at[3])]
    for copy in (bring[0], bring[2], bring[1], bring[3]):
        copy.start()
    greet(partners)
    gather = functools.partial(gather_tick, w=w, send=gsend, recv=grecv, at=at)
    bring[0].wait()
    for i in range(3):
        gather(i)
    bring[2].wait()

    def enter(rows):
        a_ref[rows, :] = normed(h_ref[rows, :])
        acc_ref[rows, :] = jnp.zeros((TILE, D), F32)

    over(TILE, enter)
    bring[1].wait()
    for i in range(3, 5):
        gather(i)

    def fetched(u, n):
        for j in range(n):
            gather(u + j + 5)
        for j in range(n):
            gather_ready(u + j, w, gsend, grecv, at)

    def forward(s, n):
        fetched(2 * s, n)
        forward_group(2 * s, n, a_ref, acc_ref, w)

    groups(forward)
    bring[3].wait()

    def between(rows):
        h = h_ref[rows, :] + acc_ref[rows, :].astype(BF)
        h_ref[rows, :] = h
        a = normed(h)
        a_ref[rows, :] = a
        a_t[:, rows] = a.T
        dy_t[:, rows] = dy_ref[rows, :].T
        acc_ref[rows, :] = jnp.zeros((TILE, D), F32)

    over(TILE, between)

    bufs = (w, r1, r2, r3)
    refs = (a_ref, a_t, dy_ref, dy_t, acc_ref, w, w_t, w_dt, dgu_ref, act_ref)

    def sent(u):
        gather_sent(u, w, gsend, grecv, at)

    def advance(stage, u, n):
        scatter_advance(stage, u, n, bufs, g_ref, ssend, srecv, at)

    def set_out(u, n):
        scatter_copy(0, u, n, bufs, ssend, srecv, at).start()

    end = UNITS - 1

    def layer1(s, n):
        u = UNITS + 2 * s
        fetched(u, n)
        backward_group(u, n, False, refs, sent)
        for stage in range(3):
            back = u - 2 - 2 * stage

            @pl.when(back >= UNITS)
            def _(stage=stage, back=back):
                advance(stage, back, 2)

        set_out(u, n)

    groups(layer1)
    again = pltpu.make_async_copy(x_ref, a_ref, sem.at[2])
    again.start()

    def leave(rows):
        wide, scale = rms(h_ref[rows, :])
        da = acc_ref[rows, :].astype(BF).astype(F32)
        along = jnp.sum(da * wide, -1, keepdims=True) * (scale * scale * scale * (1.0 / D))
        dh = dy_ref[rows, :] + (da * scale - wide * along).astype(BF)
        dy_ref[rows, :] = dh
        dy_t[:, rows] = dh.T

    over(TILE, leave)
    again.wait()

    def enter_again(rows):
        a = normed(a_ref[rows, :])
        a_ref[rows, :] = a
        a_t[:, rows] = a.T

    over(TILE, enter_again)

    def layer0(s, n):
        u = 2 * s
        backward_group(u, n, True, refs, sent)
        for stage in range(3):
            back = u - 2 - 2 * stage

            @pl.when(back >= 0)
            def _(stage=stage, back=back):
                advance(stage, back, 2)

            @pl.when(back == -2)
            def _(stage=stage):
                advance(stage, BOTH - 1, 1)

            if stage:

                @pl.when(back < -2)
                def _(stage=stage, back=back):
                    advance(stage, back + BOTH + 1, 2)

        set_out(u, n)

    groups(layer0)
    for stage, u, n in ((0, end, 1), (1, end - 2, 2), (2, end - 4, 2), (1, end, 1), (2, end - 2, 2), (2, end, 1)):
        advance(stage, u, n)
    for stage in range(3):
        for base in (UNITS, 0):

            def one(s, carry, stage=stage, base=base):
                scatter_copy(stage, base + 2 * s, 2, bufs, ssend, srecv, at).wait_send()
                return carry

            lax.fori_loop(0, GROUPS - 1, one, 0)
            scatter_copy(stage, base + end, 1, bufs, ssend, srecv, at).wait_send()


def vmem(*shape):
    return pltpu.VMEM(shape, BF)


IN_VMEM = pl.BlockSpec(memory_space=pltpu.VMEM)
ANYWHERE = pl.BlockSpec(memory_space=pl.ANY)
DMA = pltpu.SemaphoreType.DMA


def gradients_of(x, dy, own):
    return pl.pallas_call(
        kernel,
        name="both_layers",
        out_shape=jax.ShapeDtypeStruct((BOTH, 96, 256), BF),
        in_specs=[ANYWHERE] * 3,
        out_specs=IN_VMEM,
        scratch_shapes=[
            vmem(T, D),
            vmem(T, D),
            vmem(D, T),
            vmem(T, D),
            vmem(D, T),
            pltpu.VMEM((T, D), F32),
            vmem(BOTH, 2, 2, 2, 96, 256),
            vmem(512, D),
            vmem(D, 256),
            vmem(T, 512),
            vmem(T, 256),
            vmem(BOTH, 2, 2, 96, 256),
            vmem(BOTH, 2, 96, 256),
            vmem(BOTH, 96, 256),
            *[DMA((3, BOTH))] * 4,
            DMA((4,)),
        ],
        compiler_params=pltpu.CompilerParams(collective_id=0, has_side_effects=True, vmem_limit_bytes=VMEM_LIMIT),
        cost_estimate=pl.CostEstimate(flops=34 * T * D * FF, bytes_accessed=20_000_000, transcendentals=0),
    )(x, dy, own)


def to_units(w_gate, w_up, w_down):
    layers = w_gate.shape[0]
    wide = [w.reshape(layers, 64, 8, UNITS, 16).transpose(0, 3, 1, 2, 4).reshape(layers, UNITS, 64, 128) for w in (w_gate, w_up)]
    down = w_down.reshape(layers, UNITS, 16, 2, 256).transpose(0, 1, 3, 2, 4).reshape(layers, UNITS, 32, 256)
    return jnp.concatenate([jnp.concatenate(wide, -1), down], 2)


def from_units(g):
    layers = g.shape[0]
    wide = [
        g[:, :, :64, at : at + 128].reshape(layers, UNITS, 64, 8, 16).transpose(0, 2, 3, 1, 4).reshape(layers, 64, FF) for at in (0, 128)
    ]
    down = g[:, :, 64:].reshape(layers, UNITS, 2, 16, 256).transpose(0, 1, 3, 2, 4).reshape(layers, 208, D)
    return *wide, down


def adamw(w, m, v, g):
    m = 0.9 * m + 0.1 * g
    v = 0.95 * v + 0.05 * g * g
    step = m * lax.rsqrt(v + 1e-8) + 0.1 * w
    return (w - 0.02 * step).astype(BF), m, v


def solution(mesh):
    def step(x, dy, *arrays):
        weights, m, v = (arrays[i : i + 3] for i in (0, 3, 6))
        own = to_units(*weights)
        g = gradients_of(x[0], dy[0], own.reshape(BOTH, 96, 256))
        gradients = from_units(g.reshape(own.shape))
        new = [adamw(w.astype(F32), m, v, g.astype(F32)) for w, m, v, g in zip(weights, m, v, gradients, strict=True)]
        return tuple(one[which] for which in range(3) for one in new)

    states, cut = P(("rep", "dp"), None, None), P(None, "dp", None)
    return jax.shard_map(
        step,
        mesh=mesh,
        in_specs=(states, states) + (cut,) * 9,
        out_specs=(P("rep", "dp", None),) * 9,
        check_vma=False,
    )
```

time: 494 us -> 271 us (0.55); the launches traced: 486 us -> 270 us
  matrix products: 283 us -> 0 us
  Pallas kernels: 0 us -> 252 us
  waiting for transfers between devices: 153 us -> 0 us
  between operations: 14.9 us -> 0.86 us
  local copies, waits for them, and re-layouts: 19.1 us -> 9.85 us
  other arithmetic: 15.2 us -> 7.67 us
    dot_general x15 -> x0, matrix products: 283 us -> none  [the longest x5 106 us: layer(): gate = jnp.dot(a, w['w_gate'], preferred_element_type=jnp.float32)]
    pallas_call x0 -> x1, Pallas kernels: none -> 252 us  [gradients_of(): pl.pallas_call(kernel, name='both_layers', out_shape=jax.ShapeDtypeStruct...]
    reduce_scatter x6 -> x0, waiting for transfers between devices: 91.3 us -> none  [step(): lax.psum_scatter(by_w[name], 'dp', scatter_dimension=0, tiled=True)]
    all_gather x6 -> x0, waiting for transfers between devices: 60.2 us -> none  [fetched(): lax.all_gather(w[number], 'dp', axis=0, tiled=True)]
    unnamed x32 -> x20, local copies, waits for them, and re-layouts: 13.6 us -> 2.15 us
  transfers between devices with their start and end apart: 12 -> 0, of which waited for: 8 -> 0; matrix products, arithmetic and copies ran while one was open for 54% -> 0% of each run, Pallas kernels for 0% -> 0%
where the time goes in v2:
time: 271 us; the launch traced here: 270 us
  Pallas kernels  252 us (93%)
  local copies, waits for them, and re-layouts  9.85 us (4%)
  other arithmetic  7.67 us (3%)
    pallas_call x1, Pallas kernels, gradients_of(): pl.pallas_call(kernel, name='both_layers', out_shape=jax.ShapeDtypeStruct...  252 us
    convert_element_type x2, other arithmetic, adamw(): return ((w - 0.02 * step).astype(BF), m, v)  6.1 us

profile of v2, /device:TPU:0, one launch (start us, length us, event | category | flops | bytes accessed | tf_op | source)
XLA Modules:
  0.0 270.3 jit_solution(2949114423724147268)
XLA Ops:
  0.6 0.0 copy-start
  0.7 1.2 reshape.61
  1.8 0.1 copy.56
  1.9 0.0 copy-done
  1.9 0.4 copy.50
  2.3 0.0 copy-start.2
  2.3 0.2 copy.51
  2.5 0.3 copy.54
  2.9 0.4 copy-done.2
  3.3 0.4 copy.52
  3.7 0.2 copy.53
  4.0 0.3 copy.55
  4.3 1.2 pad_maximum_fusion.own
  5.5 251.9 %both_layers.1 = bf16[26,96,256]{2,1,0:T(8,128)(2,1)} custom-call(bf16[4096,512]{1,0:T(8,128)(2,1)} %bitcast.42, bf16[4096,512]{1,0:T(8,128)(2,1)} %bitcast.43, bf16[26,96,256]{2,1,0:T(8,128)(2,1)} %pad_maximum_fusion.own), custom_call_target="tpu_custom_call" | custom-call | flops 118648471552 | bytes 20000000 | tf_op jit(solution)/shard_map/both_layers/pallas_call | solution.py:340
  257.4 1.0 slice.14
  258.5 1.2 fusion.15
  259.7 0.3 copy.71
  260.0 1.6 reshape.65
  261.6 0.4 copy.69
  262.1 0.2 convert_bitcast_fusion
  262.3 0.1 copy.63
  262.4 0.5 copy.64
  262.9 0.4 copy.68
  263.3 0.2 convert_bitcast_fusion.1
  263.5 0.1 copy.58
  263.6 0.5 copy.59
  264.1 0.0 copy-start.1
  264.1 0.0 copy-start.3
  264.1 0.0 copy-start.4
  264.1 0.0 copy-start.5
  264.1 0.0 copy-start.6
  264.2 0.0 copy-start.7
  264.2 3.5 %fusion.8 = (bf16[2,208,512]{2,1,0:T(8,128)(2,1)}, f32[2,208,512]{2,1,0:T(8,128)}, f32[2,208,512]{2,1,0:T(8,128)}) fusion(bf16[2,208,512]{2,1,0:T(8,128)(2,1)} %param.15, f32[2,208,512]{2,1,0:T(8,128)} %reshape.65, f32[2,208,512]{2,1,0:T(8,128)} %param.21, f32[2,208,512]{2,1,0:T(8,128)} %param.18), kind=kLoop, calls=%fused_computation.20 | loop fusion | flops 3194880 | bytes 5111808 | tf_op jit(solution)/shard_map/convert_element_type | solution.py:389
  267.7 0.0 copy-done.1
  267.7 0.0 copy-done.3
  267.7 0.0 copy-done.4
  267.7 0.0 copy-done.5
  267.7 0.0 copy-done.6
  267.8 0.0 copy-done.7
  267.8 2.6 fusion.2
Async XLA Ops:
  0.6 1.2 copy-start
  2.3 1.0 copy-start.2
  264.1 3.6 %copy-start.1 = (bf16[2,64,1664]{2,1,0:T(8,128)(2,1)S(1)}, bf16[2,64,1664]{2,1,0:T(8,128)(2,1)}, u32[]{:S(2)}) copy-start(bf16[2,64,1664]{2,1,0:T(8,128)(2,1)} %param.13) | copy-start | bytes 1277956
  264.1 3.6 %copy-start.3 = (bf16[2,64,1664]{2,1,0:T(8,128)(2,1)S(1)}, bf16[2,64,1664]{2,1,0:T(8,128)(2,1)}, u32[]{:S(2)}) copy-start(bf16[2,64,1664]{2,1,0:T(8,128)(2,1)} %param.14) | copy-start | bytes 1277956
  264.1 3.6 %copy-start.4 = (f32[2,64,1664]{2,1,0:T(8,128)S(1)}, f32[2,64,1664]{2,1,0:T(8,128)}, u32[]{:S(2)}) copy-start(f32[2,64,1664]{2,1,0:T(8,128)} %param.19) | copy-start | bytes 2555908
  264.1 3.6 %copy-start.5 = (f32[2,64,1664]{2,1,0:T(8,128)S(1)}, f32[2,64,1664]{2,1,0:T(8,128)}, u32[]{:S(2)}) copy-start(f32[2,64,1664]{2,1,0:T(8,128)} %param.16) | copy-start | bytes 2555908
  264.1 3.6 %copy-start.6 = (f32[2,64,1664]{2,1,0:T(8,128)S(1)}, f32[2,64,1664]{2,1,0:T(8,128)}, u32[]{:S(2)}) copy-start(f32[2,64,1664]{2,1,0:T(8,128)} %param.20) | copy-start | bytes 2555908
  264.2 3.6 %copy-start.7 = (f32[2,64,1664]{2,1,0:T(8,128)S(1)}, f32[2,64,1664]{2,1,0:T(8,128)}, u32[]{:S(2)}) copy-start(f32[2,64,1664]{2,1,0:T(8,128)} %param.17) | copy-start | bytes 2555908

commit v3 on v2

--- a/solution.py
+++ b/solution.py
@@ -10,7 +10,9 @@
 T, D, FF = 4096, 512, 1664
 UNITS = 13
 GROUPS = 7
-TILE = 512
+TILE = 1024
+ROWS = 512
+PAIRS = UNITS
 VMEM_LIMIT = 67_043_328
 BF, F32 = jnp.bfloat16, jnp.float32
 BOTH = 2 * UNITS
@@ -30,58 +32,97 @@
 
 
 def place():
-    me = lax.axis_index("dp")
+    me, rep = lax.axis_index("dp"), lax.axis_index("rep")
     z1, z0, c = lax.div(me, 4), lax.rem(lax.div(me, 2), 2), lax.rem(me, 2)
-    return z1, z0, c, (me + 1 - 2 * c, me + 2 - 4 * z0, me + 4 - 8 * z1)
-
-
-def greet(partners):
+    x, y = lax.div(rep, 2), lax.rem(rep, 2)
+    return z1, z0, c, (me + 1 - 2 * c, me + 2 - 4 * z0, me + 4 - 8 * z1), (x, y), (rep + 2 - 4 * x, rep + 1 - 2 * y)
+
+
+def greet(at):
     barrier = pltpu.get_barrier_semaphore()
-    for p in partners:
-        pl.semaphore_signal(barrier, inc=1, device_id={"dp": p}, device_id_type=pl.DeviceIdType.MESH)
-    pl.semaphore_wait(barrier, 3)
+    for axis, partners in (("dp", at[3]), ("rep", at[5])):
+        for p in partners:
+            pl.semaphore_signal(barrier, inc=1, device_id={axis: p}, device_id_type=pl.DeviceIdType.MESH)
+    pl.semaphore_wait(barrier, 5)
+
+
+def turn(i, of):
+    return of[0] + lax.rem(i, 2) * (of[1] - of[0])
+
+
+def mine_of(i, at):
+    return 2 * i + turn(i, at[4])
 
 
 def gather_copy(stage, u, w, send, recv, at):
-    z1, z0, c, partners = at
-    ref = (w.at[u, z1, z0, c], w.at[u, :, z0, c], w.at[u, :, :, c])[stage]
+    z1, z0, c, partners, _, sides = at
+    ref = (w.at[u, z1, z0, c], w.at[u, :, z0, c], w.at[u, :, :, c], w.at[u, :, :, c])[stage]
+    to = ({"dp": partners[2]}, {"dp": partners[1]}, {"rep": turn(lax.div(u, 2), sides)}, {"dp": partners[0]})[stage]
     return pltpu.make_async_remote_copy(
         src_ref=ref,
         dst_ref=ref,
         send_sem=send.at[stage, u],
         recv_sem=recv.at[stage, u],
-        device_id={"dp": partners[2 - stage]},
+        device_id=to,
         device_id_type=pl.DeviceIdType.MESH,
     )
 
 
 def gather_tick(i, w, send, recv, at):
-    @pl.when(i < BOTH)
+    def copy(stage, u):
+        return gather_copy(stage, u, w, send, recv, at)
+
+    @pl.when(i < PAIRS)
     def _():
-        gather_copy(0, i, w, send, recv, at).start()
-
-    @pl.when((i >= 2) & (i < BOTH + 2))
+        copy(0, mine_of(i, at)).start()
+
+    @pl.when((i >= 2) & (i < PAIRS + 1))
     def _():
-        gather_copy(0, i - 2, w, send, recv, at).wait_recv()
-        gather_copy(1, i - 2, w, send, recv, at).start()
-
-    @pl.when((i >= 4) & (i < BOTH + 4))
+        u = mine_of(i - 1, at)
+        copy(0, u).wait_recv()
+        copy(1, u).start()
+
+    @pl.when((i >= 3) & (i < PAIRS + 2))
     def _():
-        gather_copy(1, i - 4, w, send, recv, at).wait_recv()
-        gather_copy(2, i - 4, w, send, recv, at).start()
+        u = mine_of(i - 2, at)
+        copy(1, u).wait_recv()
+        copy(2, u).start()
+        copy(3, u).start()
+
+    @pl.when((i >= 4) & (i < PAIRS + 3))
+    def _():
+        u = 4 * (i - 3) + 1 - mine_of(i - 3, at)
+        copy(2, u).wait_recv()
+        copy(3, u).start()
+
+
+def gather_first(tick, w, send, recv, at):
+    for stage in range(3):
+        for u in range(2):
+            if stage:
+                gather_copy(stage - 1, u, w, send, recv, at).wait_recv()
+            gather_copy(stage + stage // 2, u, w, send, recv, at).start()
+        tick(stage + 1)
 
 
 def gather_ready(u, w, send, recv, at):
-    gather_copy(2, u, w, send, recv, at).wait_recv()
+    gather_copy(3, u, w, send, recv, at).wait_recv()
 
 
 def gather_sent(u, w, send, recv, at):
-    for stage in range(3):
-        gather_copy(stage, u, w, send, recv, at).wait_send()
+    i = lax.div(u, 2)
+    mine = u == mine_of(i, at)
+    for stage, sent in ((0, mine | (i == 0)), (1, mine | (i == 0)), (2, mine & (i > 0))):
+
+        @pl.when(sent)
+        def _(stage=stage):
+            gather_copy(stage, u, w, send, recv, at).wait_send()
+
+    gather_copy(3, u, w, send, recv, at).wait_send()
 
 
 def scatter_copy(stage, u, n, bufs, send, recv, at):
-    z1, z0, c, partners = at
+    z1, z0, c, partners = at[:4]
     own, r1, r2, r3 = bufs
     us = pl.ds(u, n)
     src = (own.at[us, :, :, 1 - c], r1.at[us, :, 1 - z0], r2.at[us, 1 - z1])[stage]
@@ -97,7 +138,7 @@
 
 
 def scatter_advance(stage, u, n, bufs, g_ref, send, recv, at):
-    z1, z0, c, partners = at
+    z1, z0, c, partners = at[:4]
     own, r1, r2, r3 = bufs
     scatter_copy(stage, u, n, bufs, send, recv, at).wait_recv()
     for v in range(n):
@@ -193,43 +234,47 @@
 
 
 def kernel(
-    x_ref, dy_in, own, g_ref, h_ref, a_ref, a_t, dy_ref, dy_t, acc_ref, w, w_t, w_dt, dgu_ref, act_ref, r1, r2, r3, gsend, grecv, ssend, srecv, sem
+    x_ref, dy_in, own, g_ref, a_kept, a_t_kept, h_ref, a_ref, a_t, dy_ref, dy_t, acc_ref, w, w_t, w_dt, dgu_ref, act_ref, r1, r2, r3, gsend, grecv, ssend, srecv, sem
 ):
     at = place()
-    z1, z0, c, partners = at
+    z1, z0, c, partners = at[:4]
     halves = [pl.ds(0, UNITS), pl.ds(UNITS, UNITS)]
     bring = [pltpu.make_async_copy(own.at[us], w.at[us, z1, z0, c], sem.at[i]) for i, us in enumerate(halves)]
     bring += [pltpu.make_async_copy(x_ref, h_ref, sem.at[2]), pltpu.make_async_copy(dy_in, dy_ref, sem.at[3])]
-    for copy in (bring[0], bring[2], bring[1], bring[3]):
+    for copy in bring:
         copy.start()
-    greet(partners)
+    bring[0].wait()
+    bring[1].wait()
+    greet(at)
     gather = functools.partial(gather_tick, w=w, send=gsend, recv=grecv, at=at)
-    bring[0].wait()
-    for i in range(3):
+    gather_first(gather, w, gsend, grecv, at)
+    bring[2].wait()
+    bring[3].wait()
+
+    def enter(rows):
+        a = normed(h_ref[rows, :])
+        a_ref[rows, :] = a
+        a_t[:, rows] = a.T
+        dy_t[:, rows] = dy_ref[rows, :].T
+        acc_ref[rows, :] = jnp.zeros((ROWS, D), F32)
+
+    over(ROWS, enter)
+    keep = [pltpu.make_async_copy(a_ref, a_kept, sem.at[0]), pltpu.make_async_copy(a_t, a_t_kept, sem.at[1])]
+    for copy in keep:
+        copy.start()
+
+    def fetched(i, u, n):
         gather(i)
-    bring[2].wait()
-
-    def enter(rows):
-        a_ref[rows, :] = normed(h_ref[rows, :])
-        acc_ref[rows, :] = jnp.zeros((TILE, D), F32)
-
-    over(TILE, enter)
-    bring[1].wait()
-    for i in range(3, 5):
-        gather(i)
-
-    def fetched(u, n):
-        for j in range(n):
-            gather(u + j + 5)
         for j in range(n):
             gather_ready(u + j, w, gsend, grecv, at)
 
     def forward(s, n):
-        fetched(2 * s, n)
+        fetched(s + 4, 2 * s, n)
         forward_group(2 * s, n, a_ref, acc_ref, w)
 
     groups(forward)
-    bring[3].wait()
+    for copy in keep:
+        copy.wait()
 
     def between(rows):
         h = h_ref[rows, :] + acc_ref[rows, :].astype(BF)
@@ -237,10 +282,9 @@
         a = normed(h)
         a_ref[rows, :] = a
         a_t[:, rows] = a.T
-        dy_t[:, rows] = dy_ref[rows, :].T
-        acc_ref[rows, :] = jnp.zeros((TILE, D), F32)
-
-    over(TILE, between)
+        acc_ref[rows, :] = jnp.zeros((ROWS, D), F32)
+
+    over(ROWS, between)
 
     bufs = (w, r1, r2, r3)
     refs = (a_ref, a_t, dy_ref, dy_t, acc_ref, w, w_t, w_dt, dgu_ref, act_ref)
@@ -258,7 +302,7 @@
 
     def layer1(s, n):
         u = UNITS + 2 * s
-        fetched(u, n)
+        fetched(s + GROUPS + 4, u, n)
         backward_group(u, n, False, refs, sent)
         for stage in range(3):
             back = u - 2 - 2 * stage
@@ -270,8 +314,9 @@
         set_out(u, n)
 
     groups(layer1)
-    again = pltpu.make_async_copy(x_ref, a_ref, sem.at[2])
-    again.start()
+    again = [pltpu.make_async_copy(a_kept, a_ref, sem.at[0]), pltpu.make_async_copy(a_t_kept, a_t, sem.at[1])]
+    for copy in again:
+        copy.start()
 
     def leave(rows):
         wide, scale = rms(h_ref[rows, :])
@@ -281,15 +326,9 @@
         dy_ref[rows, :] = dh
         dy_t[:, rows] = dh.T
 
-    over(TILE, leave)
-    again.wait()
-
-    def enter_again(rows):
-        a = normed(a_ref[rows, :])
-        a_ref[rows, :] = a
-        a_t[:, rows] = a.T
-
-    over(TILE, enter_again)
+    over(ROWS, leave)
+    for copy in again:
+        copy.wait()
 
     def layer0(s, n):
         u = 2 * s
@@ -340,9 +379,9 @@
     return pl.pallas_call(
         kernel,
         name="both_layers",
-        out_shape=jax.ShapeDtypeStruct((BOTH, 96, 256), BF),
+        out_shape=[jax.ShapeDtypeStruct(dims, BF) for dims in ((BOTH, 96, 256), (T, D), (D, T))],
         in_specs=[ANYWHERE] * 3,
-        out_specs=IN_VMEM,
+        out_specs=[IN_VMEM, ANYWHERE, ANYWHERE],
         scratch_shapes=[
             vmem(T, D),
             vmem(T, D),
@@ -358,12 +397,13 @@
             vmem(BOTH, 2, 2, 96, 256),
             vmem(BOTH, 2, 96, 256),
             vmem(BOTH, 96, 256),
-            *[DMA((3, BOTH))] * 4,
+            *[DMA((4, BOTH))] * 2,
+            *[DMA((3, BOTH))] * 2,
             DMA((4,)),
         ],
         compiler_params=pltpu.CompilerParams(collective_id=0, has_side_effects=True, vmem_limit_bytes=VMEM_LIMIT),
         cost_estimate=pl.CostEstimate(flops=34 * T * D * FF, bytes_accessed=20_000_000, transcendentals=0),
-    )(x, dy, own)
+    )(x, dy, own)[0]
 
 
 def to_units(w_gate, w_up, w_down):

time: 271 us -> 239 us (0.88)
  Pallas kernels: 252 us -> 221 us
    pallas_call x1, Pallas kernels: 252 us -> 221 us  [gradients_of(): pl.pallas_call(kernel, name='both_layers', out_shape=[jax.ShapeDtypeStruc...]
where the time goes in v3:
time: 239 us
  Pallas kernels  221 us (92%)
  local copies, waits for them, and re-layouts  9.85 us (4%)
  other arithmetic  7.76 us (3%)
    pallas_call x1, Pallas kernels, gradients_of(): pl.pallas_call(kernel, name='both_layers', out_shape=[jax.ShapeDtypeStruc...  221 us
    convert_element_type x2, other arithmetic, adamw(): return ((w - 0.02 * step).astype(BF), m, v)  6.1 us

profile of v3, /device:TPU:0, one launch (start us, length us, event | category | flops | bytes accessed | tf_op | source)
XLA Modules:
  0.0 239.2 jit_solution(10098672738172585738)
XLA Ops:
  0.6 0.0 copy-start
  0.7 1.2 reshape.61
  1.8 0.1 copy.56
  1.9 0.0 copy-done
  1.9 0.4 copy.50
  2.3 0.0 copy-start.2
  2.3 0.2 copy.51
  2.5 0.3 copy.54
  2.9 0.4 copy-done.2
  3.3 0.4 copy.52
  3.7 0.2 copy.53
  4.0 0.3 copy.55
  4.3 1.3 pad_maximum_fusion.own
  5.6 220.7 %both_layers.1 = (bf16[26,96,256]{2,1,0:T(8,128)(2,1)}, bf16[4096,512]{1,0:T(8,128)(2,1)}, bf16[512,4096]{1,0:T(8,128)(2,1)}) custom-call(bf16[4096,512]{1,0:T(8,128)(2,1)} %bitcast.42, bf16[4096,512]{1,0:T(8,128)(2,1)} %bitcast.43, bf16[26,96,256]{2,1,0:T(8,128)(2,1)} %pad_maximum_fusion.own), custom_call_target="tpu_custom_call" | custom-call | flops 118648471552 | bytes 20000000 | tf_op jit(solution)/shard_map/both_layers/pallas_call | solution.py:379
  226.3 1.0 slice.14
  227.4 1.2 fusion.15
  228.6 0.3 copy.71
  228.9 1.6 reshape.65
  230.5 0.4 copy.69
  230.9 0.2 convert_bitcast_fusion
  231.1 0.1 copy.63
  231.2 0.5 copy.64
  231.7 0.4 copy.68
  232.2 0.2 convert_bitcast_fusion.1
  232.4 0.1 copy.58
  232.5 0.5 copy.59
  233.0 0.0 copy-start.1
  233.0 0.0 copy-start.3
  233.0 0.0 copy-start.4
  233.0 0.0 copy-start.5
  233.0 0.0 copy-start.6
  233.0 0.0 copy-start.7
  233.0 3.5 %fusion.8 = (bf16[2,208,512]{2,1,0:T(8,128)(2,1)}, f32[2,208,512]{2,1,0:T(8,128)}, f32[2,208,512]{2,1,0:T(8,128)}) fusion(bf16[2,208,512]{2,1,0:T(8,128)(2,1)} %param.15, f32[2,208,512]{2,1,0:T(8,128)} %reshape.65, f32[2,208,512]{2,1,0:T(8,128)} %param.21, f32[2,208,512]{2,1,0:T(8,128)} %param.18), kind=kLoop, calls=%fused_computation.20 | loop fusion | flops 3194880 | bytes 5111808 | tf_op jit(solution)/shard_map/convert_element_type | solution.py:429
  236.6 0.0 copy-done.1
  236.6 0.0 copy-done.3
  236.6 0.0 copy-done.4
  236.6 0.0 copy-done.5
  236.6 0.0 copy-done.6
  236.6 0.0 copy-done.7
  236.6 2.6 %fusion.2 = (bf16[2,64,1664]{2,1,0:T(8,128)(2,1)}, f32[2,64,1664]{2,1,0:T(8,128)}, f32[2,64,1664]{2,1,0:T(8,128)}, bf16[2,64,1664]{2,1,0:T(8,128)(2,1)}, f32[2,64,1664]{2,1,0:T(8,128)}, /*index=5*/f32[2,64,1664]{2,1,0:T(8,128)}) fusion(bf16[2,64,1664]{2,1,0:T(8,128)(2,1)S(1)} %copy-done.1, f32[2,64,1664]{2,1,0:T(8,128)S(1)} %copy.59, ...), kind=kLoop, calls=%fused_computation.14 | loop fusion | flops 6389760 | bytes 10223616 | tf_op jit(solution)/shard_map/convert_element_type | solution.py:429
Async XLA Ops:
  0.6 1.2 copy-start
  2.3 1.0 copy-start.2
  233.0 3.6 %copy-start.1 = (bf16[2,64,1664]{2,1,0:T(8,128)(2,1)S(1)}, bf16[2,64,1664]{2,1,0:T(8,128)(2,1)}, u32[]{:S(2)}) copy-start(bf16[2,64,1664]{2,1,0:T(8,128)(2,1)} %param.13) | copy-start | bytes 1277956
  233.0 3.6 %copy-start.3 = (bf16[2,64,1664]{2,1,0:T(8,128)(2,1)S(1)}, bf16[2,64,1664]{2,1,0:T(8,128)(2,1)}, u32[]{:S(2)}) copy-start(bf16[2,64,1664]{2,1,0:T(8,128)(2,1)} %param.14) | copy-start | bytes 1277956
  233.0 3.6 %copy-start.4 = (f32[2,64,1664]{2,1,0:T(8,128)S(1)}, f32[2,64,1664]{2,1,0:T(8,128)}, u32[]{:S(2)}) copy-start(f32[2,64,1664]{2,1,0:T(8,128)} %param.19) | copy-start | bytes 2555908
  233.0 3.6 %copy-start.5 = (f32[2,64,1664]{2,1,0:T(8,128)S(1)}, f32[2,64,1664]{2,1,0:T(8,128)}, u32[]{:S(2)}) copy-start(f32[2,64,1664]{2,1,0:T(8,128)} %param.16) | copy-start | bytes 2555908
  233.0 3.6 %copy-start.6 = (f32[2,64,1664]{2,1,0:T(8,128)S(1)}, f32[2,64,1664]{2,1,0:T(8,128)}, u32[]{:S(2)}) copy-start(f32[2,64,1664]{2,1,0:T(8,128)} %param.20) | copy-start | bytes 2555908
  233.0 3.6 %copy-start.7 = (f32[2,64,1664]{2,1,0:T(8,128)S(1)}, f32[2,64,1664]{2,1,0:T(8,128)}, u32[]{:S(2)}) copy-start(f32[2,64,1664]{2,1,0:T(8,128)} %param.17) | copy-start | bytes 2555908

commit v4 on v3

--- a/solution.py
+++ b/solution.py
@@ -10,7 +10,8 @@
 T, D, FF = 4096, 512, 1664
 UNITS = 13
 GROUPS = 7
-TILE = 1024
+LAGS = (1, 2, 4)
+TILE = 2048
 ROWS = 512
 PAIRS = UNITS
 VMEM_LIMIT = 67_043_328
@@ -96,13 +97,14 @@
         copy(3, u).start()
 
 
-def gather_first(tick, w, send, recv, at):
+def gather_first(tick, w, send, recv, at, meanwhile):
     for stage in range(3):
         for u in range(2):
             if stage:
                 gather_copy(stage - 1, u, w, send, recv, at).wait_recv()
             gather_copy(stage + stage // 2, u, w, send, recv, at).start()
         tick(stage + 1)
+        meanwhile(stage)
 
 
 def gather_ready(u, w, send, recv, at):
@@ -178,8 +180,10 @@
     return w[pl.ds(u, n), :, :, :, 64 + 16 * half : 80 + 16 * half, :].reshape(n * 128, 256)
 
 
-def forward_group(u, n, a_ref, acc_ref, w):
-    def tile(rows):
+def forward_group(u, n, a_ref, acc_ref, w, halfway):
+    def step(t, carry):
+        pl.when(t == T // TILE // 2)(halfway)
+        rows = pl.ds(pl.multiple_of(t * TILE, TILE), TILE)
         a = a_ref[rows, :]
         act = []
         for j in range(n):
@@ -189,8 +193,9 @@
         for half in range(2):
             columns = slice(256 * half, 256 * half + 256)
             acc_ref[rows, columns] += dot(act, w_d_of(w, u, n, half))
-
-    over(TILE, tile)
+        return carry
+
+    lax.fori_loop(0, T // TILE, step, 0)
 
 
 def backward_group(u, n, first, refs, sent):
@@ -247,30 +252,36 @@
     bring[1].wait()
     greet(at)
     gather = functools.partial(gather_tick, w=w, send=gsend, recv=grecv, at=at)
-    gather_first(gather, w, gsend, grecv, at)
-    bring[2].wait()
-    bring[3].wait()
-
-    def enter(rows):
+
+    def enter(t, carry):
+        rows = pl.ds(pl.multiple_of(t * ROWS, ROWS), ROWS)
         a = normed(h_ref[rows, :])
         a_ref[rows, :] = a
         a_t[:, rows] = a.T
         dy_t[:, rows] = dy_ref[rows, :].T
         acc_ref[rows, :] = jnp.zeros((ROWS, D), F32)
-
-    over(ROWS, enter)
+        return carry
+
+    def meanwhile(stage):
+        if stage == 0:
+            bring[2].wait()
+            bring[3].wait()
+        if stage < 2:
+            half = T // ROWS // 2
+            lax.fori_loop(half * stage, half * stage + half, enter, 0)
+
+    gather_first(gather, w, gsend, grecv, at, meanwhile)
     keep = [pltpu.make_async_copy(a_ref, a_kept, sem.at[0]), pltpu.make_async_copy(a_t, a_t_kept, sem.at[1])]
     for copy in keep:
         copy.start()
 
-    def fetched(i, u, n):
-        gather(i)
+    def fetched(u, n):
         for j in range(n):
             gather_ready(u + j, w, gsend, grecv, at)
 
     def forward(s, n):
-        fetched(s + 4, 2 * s, n)
-        forward_group(2 * s, n, a_ref, acc_ref, w)
+        fetched(2 * s, n)
+        forward_group(2 * s, n, a_ref, acc_ref, w, lambda: gather(s + 4))
 
     groups(forward)
     for copy in keep:
@@ -302,10 +313,11 @@
 
     def layer1(s, n):
         u = UNITS + 2 * s
-        fetched(s + GROUPS + 4, u, n)
+        gather(s + GROUPS + 4)
+        fetched(u, n)
         backward_group(u, n, False, refs, sent)
         for stage in range(3):
-            back = u - 2 - 2 * stage
+            back = u - 2 * LAGS[stage]
 
             @pl.when(back >= UNITS)
             def _(stage=stage, back=back):
@@ -334,7 +346,7 @@
         u = 2 * s
         backward_group(u, n, True, refs, sent)
         for stage in range(3):
-            back = u - 2 - 2 * stage
+            back = u - 2 * LAGS[stage]
 
             @pl.when(back >= 0)
             def _(stage=stage, back=back):
@@ -353,8 +365,8 @@
         set_out(u, n)
 
     groups(layer0)
-    for stage, u, n in ((0, end, 1), (1, end - 2, 2), (2, end - 4, 2), (1, end, 1), (2, end - 2, 2), (2, end, 1)):
-        advance(stage, u, n)
+    for stage, back in ((0, 0), (1, 2), (2, 6), (2, 4), (1, 0), (2, 2), (2, 0)):
+        advance(stage, end - back, 2 if back else 1)
     for stage in range(3):
         for base in (UNITS, 0):
 

time: 239 us -> 238 us (level)
  no operation moved by 1% of the time
where the time goes in v4:
time: 238 us; the launch traced here: 237 us
  Pallas kernels  219 us (92%)
  local copies, waits for them, and re-layouts  9.85 us (4%)
  other arithmetic  7.76 us (3%)
    pallas_call x1, Pallas kernels, gradients_of(): pl.pallas_call(kernel, name='both_layers', out_shape=[jax.ShapeDtypeStruc...  219 us
    convert_element_type x2, other arithmetic, adamw(): return ((w - 0.02 * step).astype(BF), m, v)  6.1 us

profile of v4, /device:TPU:0, one launch (start us, length us, event | category | flops | bytes accessed | tf_op | source)
XLA Modules:
  0.0 237.4 jit_solution(4962138906362862971)
XLA Ops:
  0.6 0.0 copy-start
  0.7 1.2 reshape.61
  1.8 0.1 copy.56
  1.9 0.0 copy-done
  1.9 0.4 copy.50
  2.3 0.0 copy-start.2
  2.3 0.2 copy.51
  2.5 0.3 copy.54
  2.9 0.4 copy-done.2
  3.3 0.4 copy.52
  3.7 0.2 copy.53
  4.0 0.3 copy.55
  4.3 1.3 pad_maximum_fusion.own
  5.6 218.9 %both_layers.1 = (bf16[26,96,256]{2,1,0:T(8,128)(2,1)}, bf16[4096,512]{1,0:T(8,128)(2,1)}, bf16[512,4096]{1,0:T(8,128)(2,1)}) custom-call(bf16[4096,512]{1,0:T(8,128)(2,1)} %bitcast.42, bf16[4096,512]{1,0:T(8,128)(2,1)} %bitcast.43, bf16[26,96,256]{2,1,0:T(8,128)(2,1)} %pad_maximum_fusion.own), custom_call_target="tpu_custom_call" | custom-call | flops 118648471552 | bytes 20000000 | tf_op jit(solution)/shard_map/both_layers/pallas_call | solution.py:391
  224.6 1.0 slice.14
  225.6 1.2 fusion.15
  226.8 0.3 copy.71
  227.2 1.6 reshape.65
  228.7 0.4 copy.69
  229.2 0.2 convert_bitcast_fusion
  229.4 0.1 copy.63
  229.5 0.5 copy.64
  230.0 0.4 copy.68
  230.4 0.2 convert_bitcast_fusion.1
  230.6 0.1 copy.58
  230.7 0.5 copy.59
  231.2 0.0 copy-start.1
  231.2 0.0 copy-start.3
  231.2 0.0 copy-start.4
  231.2 0.0 copy-start.5
  231.3 0.0 copy-start.6
  231.3 0.0 copy-start.7
  231.3 3.5 %fusion.8 = (bf16[2,208,512]{2,1,0:T(8,128)(2,1)}, f32[2,208,512]{2,1,0:T(8,128)}, f32[2,208,512]{2,1,0:T(8,128)}) fusion(bf16[2,208,512]{2,1,0:T(8,128)(2,1)} %param.15, f32[2,208,512]{2,1,0:T(8,128)} %reshape.65, f32[2,208,512]{2,1,0:T(8,128)} %param.21, f32[2,208,512]{2,1,0:T(8,128)} %param.18), kind=kLoop, calls=%fused_computation.20 | loop fusion | flops 3194880 | bytes 5111808 | tf_op jit(solution)/shard_map/convert_element_type | solution.py:441
  234.8 0.0 copy-done.1
  234.8 0.0 copy-done.3
  234.8 0.0 copy-done.4
  234.8 0.0 copy-done.5
  234.8 0.0 copy-done.6
  234.9 0.0 copy-done.7
  234.9 2.6 %fusion.2 = (bf16[2,64,1664]{2,1,0:T(8,128)(2,1)}, f32[2,64,1664]{2,1,0:T(8,128)}, f32[2,64,1664]{2,1,0:T(8,128)}, bf16[2,64,1664]{2,1,0:T(8,128)(2,1)}, f32[2,64,1664]{2,1,0:T(8,128)}, /*index=5*/f32[2,64,1664]{2,1,0:T(8,128)}) fusion(bf16[2,64,1664]{2,1,0:T(8,128)(2,1)S(1)} %copy-done.1, f32[2,64,1664]{2,1,0:T(8,128)S(1)} %copy.59, ...), kind=kLoop, calls=%fused_computation.14 | loop fusion | flops 6389760 | bytes 10223616 | tf_op jit(solution)/shard_map/convert_element_type | solution.py:441
Async XLA Ops:
  0.6 1.2 copy-start
  2.3 1.0 copy-start.2
  231.2 3.6 %copy-start.1 = (bf16[2,64,1664]{2,1,0:T(8,128)(2,1)S(1)}, bf16[2,64,1664]{2,1,0:T(8,128)(2,1)}, u32[]{:S(2)}) copy-start(bf16[2,64,1664]{2,1,0:T(8,128)(2,1)} %param.13) | copy-start | bytes 1277956
  231.2 3.6 %copy-start.3 = (bf16[2,64,1664]{2,1,0:T(8,128)(2,1)S(1)}, bf16[2,64,1664]{2,1,0:T(8,128)(2,1)}, u32[]{:S(2)}) copy-start(bf16[2,64,1664]{2,1,0:T(8,128)(2,1)} %param.14) | copy-start | bytes 1277956
  231.2 3.6 %copy-start.4 = (f32[2,64,1664]{2,1,0:T(8,128)S(1)}, f32[2,64,1664]{2,1,0:T(8,128)}, u32[]{:S(2)}) copy-start(f32[2,64,1664]{2,1,0:T(8,128)} %param.19) | copy-start | bytes 2555908
  231.2 3.6 %copy-start.5 = (f32[2,64,1664]{2,1,0:T(8,128)S(1)}, f32[2,64,1664]{2,1,0:T(8,128)}, u32[]{:S(2)}) copy-start(f32[2,64,1664]{2,1,0:T(8,128)} %param.16) | copy-start | bytes 2555908
  231.3 3.6 %copy-start.6 = (f32[2,64,1664]{2,1,0:T(8,128)S(1)}, f32[2,64,1664]{2,1,0:T(8,128)}, u32[]{:S(2)}) copy-start(f32[2,64,1664]{2,1,0:T(8,128)} %param.20) | copy-start | bytes 2555908
  231.3 3.6 %copy-start.7 = (f32[2,64,1664]{2,1,0:T(8,128)S(1)}, f32[2,64,1664]{2,1,0:T(8,128)}, u32[]{:S(2)}) copy-start(f32[2,64,1664]{2,1,0:T(8,128)} %param.17) | copy-start | bytes 2555908
